TPU v7x, 32 devices: a whole 2x2x4 slice. The times are simulated.
32 devices in a mesh: dp: 4 (over y, core), tensor: 8 (over z, x).
Axes of the slice: x: 2, y: 2, z: 4, core: 2. Of those that a mesh axis runs over, the one named last changes fastest.
Arguments:
- attn_input: bfloat16 [512, 8192], P('dp'), may hold values from -6 to 6
- residual: bfloat16 [512, 8192], P('dp'), may hold values from -3 to 3
- query_weight: bfloat16 [8192, 2048], P('dp', 'tensor'), may hold values from -0.0625 to 0.0625
- query_bias: bfloat16 [2048], P('tensor'), may hold values from -3 to 3
- output_weight: bfloat16 [2048, 8192], P('tensor', 'dp'), may hold values from -0.125 to 0.125
- cached_keys: bfloat16 [4, 8, 1024, 128], P('dp', 'tensor'), may hold values from -305 to 305, as said below
- cached_values: bfloat16 [4, 8, 1024, 128], P('dp', 'tensor'), may hold values from -12 to 12, as said below
- norm_gain: bfloat16 [8192], replicated, may hold values from 0.5 to 1.5
Outputs:
- hidden_out: bfloat16 [512, 8192], P(('dp', 'tensor'))
- normed_out: bfloat16 [512, 8192], P('dp')
Inputs may be any that keep to these rules, and one draw needn't show every extreme that they name: `cached_keys`: groups g and g2 with g // 1 == g2 // 1 carry equal keys. `cached_values`: groups g and g2 with g // 1 == g2 // 1 carry equal values.
All inputs are finite; a program needn't handle non-finite values.
Results may differ from a plain program's by a relative error of at most 0.025.
Values may be sent and summed in bfloat16 or wider, within the bound.
No kernel may reach another device: no remote copies, remote signals or barrier semaphores. Data moves between devices by JAX's collectives and lax.ppermute only.
A program may use at most 64 MiB of HBM per device.

v0:
```python
import jax
import jax.numpy as jnp
from jax import lax
from jax.experimental import pallas as pl
from jax.experimental.pallas import tpu as pltpu
from jax.sharding import PartitionSpec as P


rope_theta = 1000000.0
norm_eps = 1e-06


def rotate(projected, first_pos):
    head_dim = projected.shape[-1]
    half_dim = head_dim // 2
    inv_freq = jnp.power(
        jnp.float32(rope_theta), -2.0 * jnp.arange(half_dim, dtype=jnp.float32) / head_dim
    )
    positions = first_pos + jnp.arange(projected.shape[0], dtype=jnp.float32)
    angles = positions[:, None] * inv_freq[None, :]
    cosine = jnp.cos(angles)[:, None, :]
    sine = jnp.sin(angles)[:, None, :]
    first_half = projected[..., :half_dim]
    second_half = projected[..., half_dim:]
    return jnp.concatenate(
        [first_half * cosine - second_half * sine, second_half * cosine + first_half * sine],
        axis=-1,
    )


def attend(queries, local_keys, local_values):
    count_q = queries.shape[0]
    count_k = local_keys.shape[0]
    scores = jnp.einsum("thd,kd->htk", queries, local_keys, preferred_element_type=jnp.float32) * (
        1.0 / queries.shape[-1] ** 0.5
    )
    visible = jnp.arange(count_k)[None, :] <= (count_k - count_q + jnp.arange(count_q))[:, None]
    scores = jnp.where(visible[None], scores, jnp.float32(-1e30))
    highest = jnp.max(scores, axis=-1, keepdims=True)
    expo = jnp.exp(scores - highest)
    soft = (expo / jnp.sum(expo, axis=-1, keepdims=True)).astype(jnp.bfloat16)
    mixed = jnp.einsum("htk,kd->thd", soft, local_values, preferred_element_type=jnp.float32)
    return mixed.astype(jnp.bfloat16)


def normalize(total, norm_gain):
    mean_square = jnp.mean(total * total, axis=-1, keepdims=True)
    return (total * lax.rsqrt(mean_square + norm_eps) * norm_gain.astype(jnp.float32)).astype(
        jnp.bfloat16
    )


def gathered_body(
    attn_input,
    residual,
    query_weight,
    query_bias,
    output_weight,
    cached_keys,
    cached_values,
    norm_gain,
):
    tok_count = attn_input.shape[0]
    ctx_len = cached_keys.shape[2]
    head_dim = cached_keys.shape[3]
    local_heads = query_weight.shape[1] // head_dim
    projected = jnp.dot(
        attn_input,
        lax.all_gather(query_weight, "dp", axis=0, tiled=True),
        preferred_element_type=jnp.float32,
    )
    projected = projected + query_bias.astype(jnp.float32)
    queries = rotate(
        projected.reshape(tok_count, local_heads, head_dim), float(ctx_len - tok_count)
    ).astype(jnp.bfloat16)
    mixed = attend(queries, cached_keys[0, 0], cached_values[0, 0]).reshape(
        tok_count, local_heads * head_dim
    )
    partial_sum = jnp.dot(
        mixed,
        lax.all_gather(output_weight, "dp", axis=1, tiled=True),
        preferred_element_type=jnp.float32,
    )
    own_count = tok_count // lax.axis_size("tensor")
    own_start = lax.axis_index("tensor") * own_count
    summed = lax.psum(partial_sum.astype(jnp.bfloat16), "tensor").astype(jnp.float32)
    total = residual.astype(jnp.float32) + summed
    normed_out = normalize(total, norm_gain)
    hidden_out = lax.dynamic_slice_in_dim(total, own_start, own_count, 0).astype(jnp.bfloat16)
    return (hidden_out, normed_out)


def ring_order(count):
    return list(range(0, count, 2)) + list(range(count - 1, 0, -2))


def shift_in_ring(value, step):
    count = lax.axis_size("tensor")
    order = ring_order(count)
    pairs = [(order[i], order[(i + step) % count]) for i in range(count)]
    return lax.ppermute(value, "tensor", pairs)


def ring_sources(own, count):
    place = jnp.where(own % 2 == 0, own // 2, count - 1 - own // 2)
    back = [(place - k) % count for k in range(count)]
    return [jnp.where(2 * p < count, 2 * p, 2 * (count - 1 - p) + 1) for p in back]


def ring_gather(value, last_step):
    count = lax.axis_size("tensor")
    ahead, back = value, value
    found = {0: value}
    for k in range(1, (count + 1) // 2):
        ahead = shift_in_ring(ahead, 1)
        back = shift_in_ring(back, -1)
        found[k], found[count - k] = ahead, back
    found[count // 2] = shift_in_ring(ahead if last_step > 0 else back, last_step)
    return [found[k] for k in range(count)]


def pair_owners(own, count):
    return [((own ^ (k % 2)) - 2 * (k // 2)) % count for k in range(count)]


def swap_pair(value):
    count = lax.axis_size("dp")
    return lax.ppermute(value, "dp", [(i, i ^ 1) for i in range(count)])


def shift_pairs(value):
    count = lax.axis_size("dp")
    return lax.ppermute(value, "dp", [(i, (i + 2) % count) for i in range(count)])


def pair_gather(value):
    count = lax.axis_size("dp")
    own = lax.axis_index("dp")
    found = []
    for k in range(count // 2):
        if k:
            value = shift_pairs(value)
        found.append(((own - 2 * k) % count, value))
        found.append((((own ^ 1) - 2 * k) % count, swap_pair(value)))
    return found


def finish_kernel(own_t, own_d, gain, *refs, width):
    chunks, (hidden, normed) = refs[:-2], refs[-2:]
    features = normed.shape[1]
    squares = jnp.zeros((normed.shape[0], 128), jnp.float32)
    for chunk in chunks:
        for i in range(chunk.shape[1] // 128):
            part = chunk[:, i * 128 : (i + 1) * 128].astype(jnp.float32)
            squares = squares + part * part
    scale = lax.rsqrt(jnp.sum(squares, axis=1, keepdims=True) / features + norm_eps)
    own_rows = pl.ds(pl.multiple_of(own_t[0] * hidden.shape[0], hidden.shape[0]), hidden.shape[0])
    per_chunk = chunks[0].shape[1] // width
    count_t = len(chunks) // 2
    sources = ring_sources(own_t[0], count_t)
    owners = pair_owners(own_d[0], 2 * per_chunk)
    for k, chunk in enumerate(chunks):
        for i in range(per_chunk):
            owner = owners[k % 2 * per_chunk + i]
            start = (owner * count_t + sources[k // 2]) * width
            columns = pl.ds(pl.multiple_of(start, 128), width)
            part = chunk[:, i * width : (i + 1) * width].astype(jnp.float32)
            normed[:, columns] = (part * scale * gain[:, columns].astype(jnp.float32)).astype(
                jnp.bfloat16
            )
            hidden[:, columns] = chunk[own_rows, i * width : (i + 1) * width]


def finish(chunks, own_count, norm_gain, width):
    rows = chunks[0].shape[0]
    features = norm_gain.shape[0]
    smem = pl.BlockSpec(memory_space=pltpu.SMEM)
    vmem = pl.BlockSpec(memory_space=pltpu.VMEM)
    return pl.pallas_call(
        lambda *refs: finish_kernel(*refs, width=width),
        out_shape=(
            jax.ShapeDtypeStruct((own_count, features), jnp.bfloat16),
            jax.ShapeDtypeStruct((rows, features), jnp.bfloat16),
        ),
        in_specs=[smem, smem] + [vmem] * (1 + len(chunks)),
        out_specs=(vmem, vmem),
        name="finish",
    )(
        lax.axis_index("tensor").reshape(1),
        lax.axis_index("dp").reshape(1),
        norm_gain.reshape(1, features),
        *chunks,
    )


def exchanged_body(
    attn_input,
    residual,
    query_weight,
    query_bias,
    output_weight,
    cached_keys,
    cached_values,
    norm_gain,
):
    tok_count = attn_input.shape[0]
    ctx_len = cached_keys.shape[2]
    head_dim = cached_keys.shape[3]
    local_heads = query_weight.shape[1] // head_dim
    count_t = lax.axis_size("tensor")
    own_t = lax.axis_index("tensor")
    own_rows = query_weight.shape[0]
    shard_cols = output_weight.shape[1]
    width = shard_cols // count_t

    column_weight = lax.all_to_all(output_weight, "tensor", 1, 0, tiled=True)

    projected = query_bias.astype(jnp.float32)
    for owner, shard in pair_gather(query_weight):
        part = lax.dynamic_slice_in_dim(attn_input, owner * own_rows, own_rows, 1)
        projected = projected + jnp.dot(part, shard, preferred_element_type=jnp.float32)
    queries = rotate(
        projected.reshape(tok_count, local_heads, head_dim), float(ctx_len - tok_count)
    ).astype(jnp.bfloat16)
    mixed = attend(queries, cached_keys[0, 0], cached_values[0, 0]).reshape(
        tok_count, local_heads * head_dim
    )
    head_cols = mixed.shape[1]
    gathered = jnp.zeros((tok_count, count_t * head_cols), jnp.bfloat16)
    for source, got in zip(ring_sources(own_t, count_t), ring_gather(mixed, 1)):
        gathered = lax.dynamic_update_slice_in_dim(gathered, got, source * head_cols, 1)

    blocks = []
    for owner, shard in pair_gather(column_weight):
        summed = jnp.dot(gathered, shard, preferred_element_type=jnp.float32)
        start = owner * shard_cols + own_t * width
        resid = lax.dynamic_slice_in_dim(residual, start, width, 1).astype(jnp.float32)
        blocks.append((resid + summed).astype(jnp.bfloat16))
    count = len(blocks) // 2
    parts = [jnp.concatenate(blocks[i * count : (i + 1) * count], axis=1) for i in range(2)]
    near = ring_gather(parts[0], 1)
    far = ring_gather(parts[1], -1)
    chunks = [chunk for got in zip(near, far) for chunk in got]
    return finish(chunks, tok_count // count_t, norm_gain, width)


def body(*arrays):
    output_weight = arrays[4]
    width = output_weight.shape[1] // lax.axis_size("tensor")
    if width % 128 or lax.axis_size("tensor") % 2 or lax.axis_size("dp") % 2:
        return gathered_body(*arrays)
    return exchanged_body(*arrays)


def solution(mesh):
    return jax.shard_map(
        body,
        mesh=mesh,
        in_specs=(
            P("dp", None),
            P("dp", None),
            P("dp", "tensor"),
            P("tensor"),
            P("tensor", "dp"),
            P("dp", "tensor", None, None),
            P("dp", "tensor", None, None),
            P(),
        ),
        out_specs=(P(("dp", "tensor"), None), P("dp", None)),
        check_vma=False,
    )
```

profile of v0, /device:TPU:0, one launch (start us, length us, event | category | flops | bytes accessed | tf_op | source)
XLA Modules:
  0.0 101.7 jit_solution(4381468094108204293)
XLA Ops:
  0.6 0.0 copy-start
  0.7 3.1 %collective-permute-start.1 = (bf16[2048,256]{1,0:T(8,128)(2,1)}, bf16[2048,256]{1,0:T(8,128)(2,1)}, u32[]{:S(2)}, u32[]{:S(2)}) collective-permute-start(bf16[2048,256]{1,0:T(8,128)(2,1)} %param.10), channel_id=1, source_target_pairs={{0,16},{8,24},{16,0},{24,8},{1,17},{9,25},{17,1},{25,9},{2,18},{10... | collective-permute-start | bytes 3145736 | tf_op jit(solution)/shard_map/ppermute | solution.py:133
  3.7 2.3 %copy.19 = bf16[256,2048]{0,1:T(8,128)(2,1)} copy(bf16[256,2048]{1,0:T(8,128)(2,1)} %param.12) | data formatting | bytes 2097152 | tf_op args[4]
  6.0 5.8 %all-to-all-start = ((bf16[256,8,256]{0,2,1:T(8,128)(2,1)}), bf16[256,8,256]{0,2,1:T(8,128)(2,1)S(1)}, u32[]{:S(2)}, u32[]{:S(2)}) async-start(bf16[256,8,256]{0,2,1:T(8,128)(2,1)} %bitcast.45), calls=%async_computation | async-start | bytes 2097152 | tf_op jit(solution)/shard_map/all_to_all | solution.py:216
  11.8 0.1 iota_compare_fusion
  12.0 15.2 %collective-permute-done.1 = bf16[2048,256]{1,0:T(8,128)(2,1)} collective-permute-done((bf16[2048,256]{1,0:T(8,128)(2,1)}, bf16[2048,256]{1,0:T(8,128)(2,1)}, u32[]{:S(2)}, u32[]{:S(2)}) %collective-permute-start.1) | collective-permute-done | bytes 1048608 | tf_op jit(solution)/shard_map/ppermute | solution.py:133
  27.6 1.0 multiply_cosine_fusion
  28.6 1.5 %convolution_add_fusion.6 = f32[128,256]{1,0:T(8,128)S(1)} fusion(bf16[2048,256]{1,0:T(8,128)(2,1)} %param.10, bf16[128,8192]{1,0:T(8,128)(2,1)S(1)} %copy-done, s32[]{:T(128)S(6)} %select_n.152, f32[256]{0:T(256)S(1)} %convert_element_type.38), kind=kOutput, calls=%fused_computation.13 | convolution fusion | flops 134250496 | bytes 1704964 | tf_op jit(solution)/shard_map/dot_general | solution.py:221
  30.1 1.5 %fusion.11 = f32[128,256]{1,0:T(8,128)S(1)} fusion(bf16[2048,256]{1,0:T(8,128)(2,1)} %collective-permute-done.1, bf16[128,8192]{1,0:T(8,128)(2,1)S(1)} %copy-done, s32[]{:T(128)S(6)} %select_n.156), kind=kOutput, calls=%fused_computation.21 | convolution fusion | flops 134217728 | bytes 1703940 | tf_op jit(solution)/shard_map/dot_general | solution.py:221
  31.7 1.5 %fusion.5 = f32[128,256]{1,0:T(8,128)S(1)} fusion(f32[128,256]{1,0:T(8,128)S(1)} %fusion.11, f32[128,256]{1,0:T(8,128)S(1)} %convolution_add_fusion.6, bf16[2048,256]{1,0:T(8,128)(2,1)} %collective-permute-done, bf16[128,8192]{1,0:T(8,128)(2,1)S(1)} %copy-done, s32[]{:T(128)S(6)} %select_n.154), kind=kOutput, calls=%fused_computation.12 | convolution fusion | flops 134283264 | bytes 1966084 | tf_op jit(solution)/shard_map/dot_general | solution.py:221
  33.2 4.1 %all-to-all-done = bf16[256,8,256]{0,2,1:T(8,128)(2,1)S(1)} async-done(((bf16[256,8,256]{0,2,1:T(8,128)(2,1)}), bf16[256,8,256]{0,2,1:T(8,128)(2,1)S(1)}, u32[]{:S(2)}, u32[]{:S(2)}) %all-to-all-start) | async-done | bytes 1048608 | tf_op jit(solution)/shard_map/all_to_all | solution.py:216
  37.4 1.0 copy-done.1
  38.4 1.5 %copy.20 = bf16[8,256,256]{2,1,0:T(8,128)(2,1)S(1)} copy(bf16[8,256,256]{1,2,0:T(8,128)(2,1)} %bitcast.44) | data formatting | bytes 2097152 | tf_op jit(solution)/shard_map/all_to_all | solution.py:216
  39.8 0.6 collective-permute-start.11
  40.4 1.5 %convolution_add_fusion.4 = f32[128,256]{1,0:T(8,128)S(1)} fusion(f32[128,256]{1,0:T(8,128)S(1)} %fusion.5, bf16[2048,256]{1,0:T(8,128)(2,1)} %collective-permute-done.2, bf16[128,8192]{1,0:T(8,128)(2,1)S(1)} %copy-done, s32[]{:T(128)S(6)} %select_n.158), kind=kOutput, calls=%fused_computation.10 | convolution fusion | flops 134250496 | bytes 1835012 | tf_op jit(solution)/shard_map/dot_general | solution.py:221
  42.0 0.1 reshape.107
  42.1 0.2 fusion.29
  42.3 0.9 subtract_convert_fusion
  43.2 2.3 %fusion.4 = f32[2,128,1024]{2,1,0:T(8,128)} fusion(pred[128,1024]{1,0:T(8,128)(4,1)S(1)} %iota_compare_fusion, bf16[1,1,1024,128]{3,2,1,0:T(8,128)(2,1)} %param.13, bf16[128,2,64]{2,0,1:T(8,128)(2,1)S(1)} %get-tuple-element.3, bf16[128,2,64]{2,0,1:T(8,128)(2,1)S(1)} %get-tuple-element.2), kind=kOutput, calls=%fused_computation.5 | convolution fusion | flops 67764224 | bytes 1507328 | tf_op jit(solution)/shard_map/thd,kd->htk/dot_general | solution.py:34
  45.5 1.6 %fusion.30 = f32[2,128]{1,0:T(2,128)S(1)} fusion(pred[128,1024]{1,0:T(8,128)(4,1)S(1)} %iota_compare_fusion, bf16[1,1,1024,128]{3,2,1,0:T(8,128)(2,1)} %param.13, bf16[128,2,64]{2,0,1:T(8,128)(2,1)S(1)} %get-tuple-element.3, bf16[128,2,64]{2,0,1:T(8,128)(2,1)S(1)} %get-tuple-element.2), kind=kOutput, calls=%fused_computation.56 | convolution fusion | flops 68289536 | bytes 459776 | tf_op jit(solution)/shard_map/sub | solution.py:40
  47.1 2.5 %convolution_convert_fusion = bf16[2,128,128]{1,2,0:T(8,128)(2,1)S(1)} fusion(f32[2,128]{1,0:T(2,128)S(1)} %fusion.30, bf16[1,1,1024,128]{3,2,1,0:T(8,128)(2,1)} %param.14, f32[2,128,1024]{2,1,0:T(8,128)} %fusion.4), kind=kOutput, calls=%fused_computation.18 | convolution fusion | flops 67929344 | bytes 1377280 | tf_op jit(solution)/shard_map/htk,kd->thd/dot_general | solution.py:42
  49.5 0.1 collective-permute-start.3
  49.6 2.0 %collective-permute-start.7 = (bf16[128,256]{0,1:T(8,128)(2,1)S(1)}, bf16[128,256]{0,1:T(8,128)(2,1)S(1)}, u32[]{:S(2)}, u32[]{:S(2)}) collective-permute-start(bf16[128,256]{0,1:T(8,128)(2,1)S(1)} %bitcast.47), channel_id=1, source_target_pairs={{0,1},{2,0},{4,2},{6,4},{7,6},{5,7},{3,5},{1,3},{8,9},{10,8},{12,1... | collective-permute-start | bytes 196616 | tf_op jit(solution)/shard_map/ppermute | solution.py:101
  51.6 0.1 broadcast_in_dim.10
  51.7 2.4 %collective-permute-done.3 = bf16[128,256]{0,1:T(8,128)(2,1)S(1)} collective-permute-done((bf16[128,256]{0,1:T(8,128)(2,1)S(1)}, bf16[128,256]{0,1:T(8,128)(2,1)S(1)}, u32[]{:S(2)}, u32[]{:S(2)}) %collective-permute-start.3) | collective-permute-done | bytes 65568 | tf_op jit(solution)/shard_map/ppermute | solution.py:101
  54.1 0.3 collective-permute-start.4
  54.4 1.7 %collective-permute-start.8 = (bf16[128,256]{0,1:T(8,128)(2,1)S(1)}, bf16[128,256]{0,1:T(8,128)(2,1)S(1)}, u32[]{:S(2)}, u32[]{:S(2)}) collective-permute-start(bf16[128,256]{0,1:T(8,128)(2,1)S(1)} %collective-permute-done.7), channel_id=1, source_target_pairs={{0,1},{2,0},{4,2},{6,4},{7,6},{5,7},{3,5},{1,3},{8,9},{10,8},{12,1... | collective-permute-start | bytes 196616 | tf_op jit(solution)/shard_map/ppermute | solution.py:101
  56.1 2.2 %collective-permute-done.4 = bf16[128,256]{0,1:T(8,128)(2,1)S(1)} collective-permute-done((bf16[128,256]{0,1:T(8,128)(2,1)S(1)}, bf16[128,256]{0,1:T(8,128)(2,1)S(1)}, u32[]{:S(2)}, u32[]{:S(2)}) %collective-permute-start.4) | collective-permute-done | bytes 65568 | tf_op jit(solution)/shard_map/ppermute | solution.py:101
  58.3 0.3 collective-permute-start.5
  58.6 1.7 %collective-permute-start.9 = (bf16[128,256]{0,1:T(8,128)(2,1)S(1)}, bf16[128,256]{0,1:T(8,128)(2,1)S(1)}, u32[]{:S(2)}, u32[]{:S(2)}) collective-permute-start(bf16[128,256]{0,1:T(8,128)(2,1)S(1)} %collective-permute-done.8), channel_id=1, source_target_pairs={{0,1},{2,0},{4,2},{6,4},{7,6},{5,7},{3,5},{1,3},{8,9},{10,8},{12,1... | collective-permute-start | bytes 196616 | tf_op jit(solution)/shard_map/ppermute | solution.py:101
  60.4 2.2 %collective-permute-done.5 = bf16[128,256]{0,1:T(8,128)(2,1)S(1)} collective-permute-done((bf16[128,256]{0,1:T(8,128)(2,1)S(1)}, bf16[128,256]{0,1:T(8,128)(2,1)S(1)}, u32[]{:S(2)}, u32[]{:S(2)}) %collective-permute-start.5) | collective-permute-done | bytes 65568 | tf_op jit(solution)/shard_map/ppermute | solution.py:101
  62.6 0.3 collective-permute-start.6
  62.9 4.0 %collective-permute-done.6 = bf16[128,256]{0,1:T(8,128)(2,1)S(1)} collective-permute-done((bf16[128,256]{0,1:T(8,128)(2,1)S(1)}, bf16[128,256]{0,1:T(8,128)(2,1)S(1)}, u32[]{:S(2)}, u32[]{:S(2)}) %collective-permute-start.6) | collective-permute-done | bytes 65568 | tf_op jit(solution)/shard_map/ppermute | solution.py:101
  66.9 0.1 collective-permute-start.12
  67.1 1.2 %fusion.6 = bf16[128,256]{1,0:T(8,128)(2,1)S(1)} fusion(bf16[128,2048]{0,1:T(8,128)(2,1)S(1)} %constant_dynamic-update-slice_fusion, bf16[2048,256]{1,0:T(8,128)(2,1)S(1)} %bitcast.43, bf16[128,8192]{1,0:T(8,128)(2,1)} %param.9, s32[]{:T(128)S(6)} %select_n.151), kind=kOutput, calls=%fused_computation.14 | convolution fusion | flops 134316032 | bytes 1703940 | tf_op jit(solution)/shard_map/dot_general | solution.py:235
  68.3 1.6 %fusion.7 = bf16[128,256]{1,0:T(8,128)(2,1)S(1)} fusion(bf16[128,2048]{0,1:T(8,128)(2,1)S(1)} %constant_dynamic-update-slice_fusion, bf16[2048,256]{1,0:T(8,128)(2,1)} %collective-permute-done.10, bf16[128,8192]{1,0:T(8,128)(2,1)} %param.9, s32[]{:T(128)S(6)} %select_n.188), kind=kOutput, calls=%fused_computation.15 | convolution fusion | flops 134316032 | bytes 1703940 | tf_op jit(solution)/shard_map/dot_general | solution.py:235
  70.0 0.3 collective-permute-start.13
  70.3 1.6 %fusion.8 = bf16[128,256]{1,0:T(8,128)(2,1)S(1)} fusion(bf16[128,2048]{0,1:T(8,128)(2,1)S(1)} %constant_dynamic-update-slice_fusion, bf16[2048,256]{1,0:T(8,128)(2,1)} %collective-permute-done.11, bf16[128,8192]{1,0:T(8,128)(2,1)} %param.9, s32[]{:T(128)S(6)} %select_n.189), kind=kOutput, calls=%fused_computation.16 | convolution fusion | flops 134316032 | bytes 1703940 | tf_op jit(solution)/shard_map/dot_general | solution.py:235
  71.9 1.2 %fusion.9 = bf16[128,256]{1,0:T(8,128)(2,1)S(1)} fusion(bf16[128,2048]{0,1:T(8,128)(2,1)S(1)} %constant_dynamic-update-slice_fusion, bf16[2048,256]{1,0:T(8,128)(2,1)S(1)} %collective-permute-done.12, bf16[128,8192]{1,0:T(8,128)(2,1)} %param.9, s32[]{:T(128)S(6)} %select_n.190), kind=kOutput, calls=%fused_computation.17 | convolution fusion | flops 134316032 | bytes 1703940 | tf_op jit(solution)/shard_map/dot_general | solution.py:235
  73.2 1.8 %collective-permute-start.20 = (bf16[128,512]{1,0:T(8,128)(2,1)S(1)}, bf16[128,512]{1,0:T(8,128)(2,1)S(1)}, u32[]{:S(2)}, u32[]{:S(2)}) collective-permute-start(bf16[128,512]{1,0:T(8,128)(2,1)S(1)} %pad_maximum_fusion.1.refs_4_), channel_id=1, source_target_pairs={{0,1},{2,0},{4,2},{6,4},{7,6},{5,7},{3,5},{1,3},{8,9},{10,8},{12,1... | collective-permute-start | bytes 393224 | tf_op jit(solution)/shard_map/ppermute | solution.py:101
  75.0 1.3 %collective-permute-start.24 = (bf16[128,512]{1,0:T(8,128)(2,1)S(1)}, bf16[128,512]{1,0:T(8,128)(2,1)S(1)}, u32[]{:S(2)}, u32[]{:S(2)}) collective-permute-start(bf16[128,512]{1,0:T(8,128)(2,1)S(1)} %pad_maximum_fusion.refs_3_), channel_id=1, source_target_pairs={{0,1},{2,0},{4,2},{6,4},{7,6},{5,7},{3,5},{1,3},{8,9},{10,8},{12,1... | collective-permute-start | bytes 393224 | tf_op jit(solution)/shard_map/ppermute | solution.py:101
  76.3 0.7 collective-permute-start.15
  77.0 0.3 collective-permute-start.14
  77.3 2.3 %collective-permute-done.20.refs_18_ = bf16[128,512]{1,0:T(8,128)(2,1)S(1)} collective-permute-done((bf16[128,512]{1,0:T(8,128)(2,1)S(1)}, bf16[128,512]{1,0:T(8,128)(2,1)S(1)}, u32[]{:S(2)}, u32[]{:S(2)}) %collective-permute-start.20) | collective-permute-done | bytes 131104 | tf_op jit(solution)/shard_map/ppermute | solution.py:101
  79.6 1.7 %collective-permute-start.21 = (bf16[128,512]{1,0:T(8,128)(2,1)S(1)}, bf16[128,512]{1,0:T(8,128)(2,1)S(1)}, u32[]{:S(2)}, u32[]{:S(2)}) collective-permute-start(bf16[128,512]{1,0:T(8,128)(2,1)S(1)} %collective-permute-done.20.refs_18_), channel_id=1, source_target_pairs={{0,1},{2,0},{4,2},{6,4},{7,6},{5,7},{3,5},{1,3},{8,9},{10,8},{12,1... | collective-permute-start | bytes 393224 | tf_op jit(solution)/shard_map/ppermute | solution.py:101
  81.4 1.1 %collective-permute-done.24.refs_17_ = bf16[128,512]{1,0:T(8,128)(2,1)S(1)} collective-permute-done((bf16[128,512]{1,0:T(8,128)(2,1)S(1)}, bf16[128,512]{1,0:T(8,128)(2,1)S(1)}, u32[]{:S(2)}, u32[]{:S(2)}) %collective-permute-start.24) | collective-permute-done | bytes 131104 | tf_op jit(solution)/shard_map/ppermute | solution.py:101
  82.4 1.7 %collective-permute-start.25 = (bf16[128,512]{1,0:T(8,128)(2,1)S(1)}, bf16[128,512]{1,0:T(8,128)(2,1)S(1)}, u32[]{:S(2)}, u32[]{:S(2)}) collective-permute-start(bf16[128,512]{1,0:T(8,128)(2,1)S(1)} %collective-permute-done.24.refs_17_), channel_id=1, source_target_pairs={{0,1},{2,0},{4,2},{6,4},{7,6},{5,7},{3,5},{1,3},{8,9},{10,8},{12,1... | collective-permute-start | bytes 393224 | tf_op jit(solution)/shard_map/ppermute | solution.py:101
  84.2 0.3 collective-permute-start.17
  84.5 0.4 collective-permute-start.16
  84.9 0.7 collective-permute-done.21.refs_16_
  85.5 1.8 %collective-permute-start.22 = (bf16[128,512]{1,0:T(8,128)(2,1)S(1)}, bf16[128,512]{1,0:T(8,128)(2,1)S(1)}, u32[]{:S(2)}, u32[]{:S(2)}) collective-permute-start(bf16[128,512]{1,0:T(8,128)(2,1)S(1)} %collective-permute-done.21.refs_16_), channel_id=1, source_target_pairs={{0,1},{2,0},{4,2},{6,4},{7,6},{5,7},{3,5},{1,3},{8,9},{10,8},{12,1... | collective-permute-start | bytes 393224 | tf_op jit(solution)/shard_map/ppermute | solution.py:101
  87.3 1.5 %collective-permute-done.25.refs_15_ = bf16[128,512]{1,0:T(8,128)(2,1)S(1)} collective-permute-done((bf16[128,512]{1,0:T(8,128)(2,1)S(1)}, bf16[128,512]{1,0:T(8,128)(2,1)S(1)}, u32[]{:S(2)}, u32[]{:S(2)}) %collective-permute-start.25) | collective-permute-done | bytes 131104 | tf_op jit(solution)/shard_map/ppermute | solution.py:101
  88.8 1.7 %collective-permute-start.26 = (bf16[128,512]{1,0:T(8,128)(2,1)S(1)}, bf16[128,512]{1,0:T(8,128)(2,1)S(1)}, u32[]{:S(2)}, u32[]{:S(2)}) collective-permute-start(bf16[128,512]{1,0:T(8,128)(2,1)S(1)} %collective-permute-done.25.refs_15_), channel_id=1, source_target_pairs={{0,1},{2,0},{4,2},{6,4},{7,6},{5,7},{3,5},{1,3},{8,9},{10,8},{12,1... | collective-permute-start | bytes 393224 | tf_op jit(solution)/shard_map/ppermute | solution.py:101
  90.5 0.3 collective-permute-start.19
  90.8 0.7 collective-permute-done.16.refs_8_
  91.5 0.3 collective-permute-start.18
  91.8 1.7 %collective-permute-start.23 = (bf16[128,512]{1,0:T(8,128)(2,1)S(1)}, bf16[128,512]{1,0:T(8,128)(2,1)S(1)}, u32[]{:S(2)}, u32[]{:S(2)}) collective-permute-start(bf16[128,512]{1,0:T(8,128)(2,1)S(1)} %collective-permute-done.22.refs_14_), channel_id=1, source_target_pairs={{0,1},{2,0},{4,2},{6,4},{7,6},{5,7},{3,5},{1,3},{8,9},{10,8},{12,1... | collective-permute-start | bytes 393224 | tf_op jit(solution)/shard_map/ppermute | solution.py:101
  93.5 0.6 reshape.106.refs_2_
  94.2 0.2 collective-permute-done.26.refs_13_
  94.4 1.1 %collective-permute-done.19.refs_11_ = bf16[128,512]{1,0:T(8,128)(2,1)S(1)} collective-permute-done((bf16[128,512]{1,0:T(8,128)(2,1)S(1)}, bf16[128,512]{1,0:T(8,128)(2,1)S(1)}, u32[]{:S(2)}, u32[]{:S(2)}) %collective-permute-start.19) | collective-permute-done | bytes 131104 | tf_op jit(solution)/shard_map/ppermute | solution.py:101
  95.5 1.4 %collective-permute-done.18.refs_10_ = bf16[128,512]{1,0:T(8,128)(2,1)S(1)} collective-permute-done((bf16[128,512]{1,0:T(8,128)(2,1)S(1)}, bf16[128,512]{1,0:T(8,128)(2,1)S(1)}, u32[]{:S(2)}, u32[]{:S(2)}) %collective-permute-start.18) | collective-permute-done | bytes 131104 | tf_op jit(solution)/shard_map/ppermute | solution.py:101
  97.0 0.6 copy-done.16
  97.6 0.1 copy-done.17
  97.7 4.0 %finish.1 = (bf16[16,8192]{1,0:T(8,128)(2,1)}, bf16[128,8192]{1,0:T(8,128)(2,1)}) custom-call(s32[1]{0:T(128)} %bitcast.refs_0_, s32[1]{0:T(128)} %bitcast.1.refs_1_, bf16[1,8192]{1,0:T(2,128)(2,1)} %reshape.106.refs_2_, bf16[128,512]{1,0:T(8,128)(2,1)} %copy-done.2, bf16[128,512]{1,0:T(8,128)(2,1)} %copy-done.3, bf16[128,512]{1,0:T(8,128)(2,1)} %copy-done.4, ...), custom_call_target="tpu_custom_call" | custom-call | tf_op jit(solution)/shard_map/finish/pallas_call | solution.py:179
  (67 shorter events, 0.3 us)
Async XLA Ops:
  0.6 28.0 %copy-start = (bf16[128,8192]{1,0:T(8,128)(2,1)S(1)}, bf16[128,8192]{1,0:T(8,128)(2,1)}, u32[]{:S(2)}) copy-start(bf16[128,8192]{1,0:T(8,128)(2,1)} %param.8) | copy-start | bytes 6291460
  0.6 26.9 %copy-start.19 = (bf16[256]{0:T(256)(128)(2,1)S(1)}, bf16[256]{0:T(256)(128)(2,1)}, u32[]{:S(2)}) copy-start(bf16[256]{0:T(256)(128)(2,1)} %param.11) | copy-start | bytes 1540
  0.7 26.5 %collective-permute-start.1 = (bf16[2048,256]{1,0:T(8,128)(2,1)}, bf16[2048,256]{1,0:T(8,128)(2,1)}, u32[]{:S(2)}, u32[]{:S(2)}) collective-permute-start(bf16[2048,256]{1,0:T(8,128)(2,1)} %param.10), channel_id=1, source_target_pairs={{0,16},{8,24},{16,0},{24,8},{1,17},{9,25},{17,1},{25,9},{2,18},{10... | collective-permute-start | bytes 3145736 | tf_op jit(solution)/shard_map/ppermute | solution.py:133
  6.0 31.4 %all-to-all-start = ((bf16[256,8,256]{0,2,1:T(8,128)(2,1)}), bf16[256,8,256]{0,2,1:T(8,128)(2,1)S(1)}, u32[]{:S(2)}, u32[]{:S(2)}) async-start(bf16[256,8,256]{0,2,1:T(8,128)(2,1)} %bitcast.45), calls=%async_computation | async-start | bytes 2097152 | tf_op jit(solution)/shard_map/all_to_all | solution.py:216
  11.8 19.9 %collective-permute-start = (bf16[2048,256]{1,0:T(8,128)(2,1)}, bf16[2048,256]{1,0:T(8,128)(2,1)}, u32[]{:S(2)}, u32[]{:S(2)}) collective-permute-start(bf16[2048,256]{1,0:T(8,128)(2,1)} %param.10), channel_id=1, source_target_pairs={{0,8},{8,0},{16,24},{24,16},{1,9},{9,1},{17,25},{25,17},{2,10},{10... | collective-permute-start | bytes 3145736 | tf_op jit(solution)/shard_map/ppermute | solution.py:128
  27.2 13.2 %collective-permute-start.2 = (bf16[2048,256]{1,0:T(8,128)(2,1)}, bf16[2048,256]{1,0:T(8,128)(2,1)}, u32[]{:S(2)}, u32[]{:S(2)}) collective-permute-start(bf16[2048,256]{1,0:T(8,128)(2,1)} %collective-permute-done.1), channel_id=1, source_target_pairs={{0,8},{8,0},{16,24},{24,16},{1,9},{9,1},{17,25},{25,17},{2,10},{10... | collective-permute-start | bytes 3145736 | tf_op jit(solution)/shard_map/ppermute | solution.py:128
  37.4 1.0 copy-start.1
  39.8 27.1 %collective-permute-start.11 = (bf16[2048,256]{1,0:T(8,128)(2,1)S(1)}, bf16[2048,256]{1,0:T(8,128)(2,1)}, u32[]{:S(2)}, u32[]{:S(2)}) collective-permute-start(bf16[2048,256]{1,0:T(8,128)(2,1)S(1)} %bitcast.41), channel_id=1, source_target_pairs={{0,16},{8,24},{16,0},{24,8},{1,17},{9,25},{17,1},{25,9},{2,18},{10... | collective-permute-start | bytes 3145736 | tf_op jit(solution)/shard_map/ppermute | solution.py:133
  40.4 27.9 %collective-permute-start.10 = (bf16[2048,256]{1,0:T(8,128)(2,1)S(1)}, bf16[2048,256]{1,0:T(8,128)(2,1)}, u32[]{:S(2)}, u32[]{:S(2)}) collective-permute-start(bf16[2048,256]{1,0:T(8,128)(2,1)S(1)} %bitcast.42), channel_id=1, source_target_pairs={{0,8},{8,0},{16,24},{24,16},{1,9},{9,1},{17,25},{25,17},{2,10},{10... | collective-permute-start | bytes 3145736 | tf_op jit(solution)/shard_map/ppermute | solution.py:128
  49.5 4.6 %collective-permute-start.3 = (bf16[128,256]{0,1:T(8,128)(2,1)S(1)}, bf16[128,256]{0,1:T(8,128)(2,1)S(1)}, u32[]{:S(2)}, u32[]{:S(2)}) collective-permute-start(bf16[128,256]{0,1:T(8,128)(2,1)S(1)} %bitcast.46), channel_id=1, source_target_pairs={{0,2},{2,4},{4,6},{6,7},{7,5},{5,3},{3,1},{1,0},{8,10},{10,12},{12... | collective-permute-start | bytes 196616 | tf_op jit(solution)/shard_map/ppermute | solution.py:101
  49.6 4.8 %collective-permute-start.7 = (bf16[128,256]{0,1:T(8,128)(2,1)S(1)}, bf16[128,256]{0,1:T(8,128)(2,1)S(1)}, u32[]{:S(2)}, u32[]{:S(2)}) collective-permute-start(bf16[128,256]{0,1:T(8,128)(2,1)S(1)} %bitcast.47), channel_id=1, source_target_pairs={{0,1},{2,0},{4,2},{6,4},{7,6},{5,7},{3,5},{1,3},{8,9},{10,8},{12,1... | collective-permute-start | bytes 196616 | tf_op jit(solution)/shard_map/ppermute | solution.py:101
  54.1 4.3 %collective-permute-start.4 = (bf16[128,256]{0,1:T(8,128)(2,1)S(1)}, bf16[128,256]{0,1:T(8,128)(2,1)S(1)}, u32[]{:S(2)}, u32[]{:S(2)}) collective-permute-start(bf16[128,256]{0,1:T(8,128)(2,1)S(1)} %collective-permute-done.3), channel_id=1, source_target_pairs={{0,2},{2,4},{4,6},{6,7},{7,5},{5,3},{3,1},{1,0},{8,10},{10,12},{12... | collective-permute-start | bytes 196616 | tf_op jit(solution)/shard_map/ppermute | solution.py:101
  54.4 4.3 %collective-permute-start.8 = (bf16[128,256]{0,1:T(8,128)(2,1)S(1)}, bf16[128,256]{0,1:T(8,128)(2,1)S(1)}, u32[]{:S(2)}, u32[]{:S(2)}) collective-permute-start(bf16[128,256]{0,1:T(8,128)(2,1)S(1)} %collective-permute-done.7), channel_id=1, source_target_pairs={{0,1},{2,0},{4,2},{6,4},{7,6},{5,7},{3,5},{1,3},{8,9},{10,8},{12,1... | collective-permute-start | bytes 196616 | tf_op jit(solution)/shard_map/ppermute | solution.py:101
  58.3 4.3 %collective-permute-start.5 = (bf16[128,256]{0,1:T(8,128)(2,1)S(1)}, bf16[128,256]{0,1:T(8,128)(2,1)S(1)}, u32[]{:S(2)}, u32[]{:S(2)}) collective-permute-start(bf16[128,256]{0,1:T(8,128)(2,1)S(1)} %collective-permute-done.4), channel_id=1, source_target_pairs={{0,2},{2,4},{4,6},{6,7},{7,5},{5,3},{3,1},{1,0},{8,10},{10,12},{12... | collective-permute-start | bytes 196616 | tf_op jit(solution)/shard_map/ppermute | solution.py:101
  58.6 8.3 %collective-permute-start.9 = (bf16[128,256]{0,1:T(8,128)(2,1)S(1)}, bf16[128,256]{0,1:T(8,128)(2,1)S(1)}, u32[]{:S(2)}, u32[]{:S(2)}) collective-permute-start(bf16[128,256]{0,1:T(8,128)(2,1)S(1)} %collective-permute-done.8), channel_id=1, source_target_pairs={{0,1},{2,0},{4,2},{6,4},{7,6},{5,7},{3,5},{1,3},{8,9},{10,8},{12,1... | collective-permute-start | bytes 196616 | tf_op jit(solution)/shard_map/ppermute | solution.py:101
  62.6 4.3 %collective-permute-start.6 = (bf16[128,256]{0,1:T(8,128)(2,1)S(1)}, bf16[128,256]{0,1:T(8,128)(2,1)S(1)}, u32[]{:S(2)}, u32[]{:S(2)}) collective-permute-start(bf16[128,256]{0,1:T(8,128)(2,1)S(1)} %collective-permute-done.5), channel_id=1, source_target_pairs={{0,2},{2,4},{4,6},{6,7},{7,5},{5,3},{3,1},{1,0},{8,10},{10,12},{12... | collective-permute-start | bytes 196616 | tf_op jit(solution)/shard_map/ppermute | solution.py:101
  66.9 5.0 %collective-permute-start.12 = (bf16[2048,256]{1,0:T(8,128)(2,1)}, bf16[2048,256]{1,0:T(8,128)(2,1)S(1)}, u32[]{:S(2)}, u32[]{:S(2)}) collective-permute-start(bf16[2048,256]{1,0:T(8,128)(2,1)} %collective-permute-done.11), channel_id=1, source_target_pairs={{0,8},{8,0},{16,24},{24,16},{1,9},{9,1},{17,25},{25,17},{2,10},{10... | collective-permute-start | bytes 3145736 | tf_op jit(solution)/shard_map/ppermute | solution.py:128
  69.9 23.6 %copy-start.18 = (bf16[8192]{0:T(1024)(128)(2,1)S(1)}, bf16[8192]{0:T(1024)(128)(2,1)}, u32[]{:S(2)}) copy-start(bf16[8192]{0:T(1024)(128)(2,1)} %param.15) | copy-start | bytes 49156
  70.0 27.7 %copy-start.2 = (bf16[128,512]{1,0:T(8,128)(2,1)}, bf16[128,512]{1,0:T(8,128)(2,1)S(1)}, u32[]{:S(2)}) copy-start(bf16[128,512]{1,0:T(8,128)(2,1)S(1)} %pad_maximum_fusion.refs_3_) | copy-start | bytes 393220
  70.0 6.3 %collective-permute-start.13 = (bf16[128,512]{1,0:T(8,128)(2,1)S(1)}, bf16[128,512]{1,0:T(8,128)(2,1)S(1)}, u32[]{:S(2)}, u32[]{:S(2)}) collective-permute-start(bf16[128,512]{1,0:T(8,128)(2,1)S(1)} %pad_maximum_fusion.refs_3_), channel_id=1, source_target_pairs={{0,2},{2,4},{4,6},{6,7},{7,5},{5,3},{3,1},{1,0},{8,10},{10,12},{12... | collective-permute-start | bytes 393224 | tf_op jit(solution)/shard_map/ppermute | solution.py:101
  73.2 24.5 %copy-start.3 = (bf16[128,512]{1,0:T(8,128)(2,1)}, bf16[128,512]{1,0:T(8,128)(2,1)S(1)}, u32[]{:S(2)}) copy-start(bf16[128,512]{1,0:T(8,128)(2,1)S(1)} %pad_maximum_fusion.1.refs_4_) | copy-start | bytes 393220
  73.2 6.4 %collective-permute-start.20 = (bf16[128,512]{1,0:T(8,128)(2,1)S(1)}, bf16[128,512]{1,0:T(8,128)(2,1)S(1)}, u32[]{:S(2)}, u32[]{:S(2)}) collective-permute-start(bf16[128,512]{1,0:T(8,128)(2,1)S(1)} %pad_maximum_fusion.1.refs_4_), channel_id=1, source_target_pairs={{0,1},{2,0},{4,2},{6,4},{7,6},{5,7},{3,5},{1,3},{8,9},{10,8},{12,1... | collective-permute-start | bytes 393224 | tf_op jit(solution)/shard_map/ppermute | solution.py:101
  75.0 7.4 %collective-permute-start.24 = (bf16[128,512]{1,0:T(8,128)(2,1)S(1)}, bf16[128,512]{1,0:T(8,128)(2,1)S(1)}, u32[]{:S(2)}, u32[]{:S(2)}) collective-permute-start(bf16[128,512]{1,0:T(8,128)(2,1)S(1)} %pad_maximum_fusion.refs_3_), channel_id=1, source_target_pairs={{0,1},{2,0},{4,2},{6,4},{7,6},{5,7},{3,5},{1,3},{8,9},{10,8},{12,1... | collective-permute-start | bytes 393224 | tf_op jit(solution)/shard_map/ppermute | solution.py:101
  76.3 21.4 %copy-start.4 = (bf16[128,512]{1,0:T(8,128)(2,1)}, bf16[128,512]{1,0:T(8,128)(2,1)S(1)}, u32[]{:S(2)}) copy-start(bf16[128,512]{1,0:T(8,128)(2,1)S(1)} %collective-permute-done.13.refs_5_) | copy-start | bytes 393220
  76.3 7.9 %collective-permute-start.15 = (bf16[128,512]{1,0:T(8,128)(2,1)S(1)}, bf16[128,512]{1,0:T(8,128)(2,1)S(1)}, u32[]{:S(2)}, u32[]{:S(2)}) collective-permute-start(bf16[128,512]{1,0:T(8,128)(2,1)S(1)} %collective-permute-done.13.refs_5_), channel_id=1, source_target_pairs={{0,2},{2,4},{4,6},{6,7},{7,5},{5,3},{3,1},{1,0},{8,10},{10,12},{12... | collective-permute-start | bytes 393224 | tf_op jit(solution)/shard_map/ppermute | solution.py:101
  77.0 7.4 %collective-permute-start.14 = (bf16[128,512]{1,0:T(8,128)(2,1)S(1)}, bf16[128,512]{1,0:T(8,128)(2,1)S(1)}, u32[]{:S(2)}, u32[]{:S(2)}) collective-permute-start(bf16[128,512]{1,0:T(8,128)(2,1)S(1)} %pad_maximum_fusion.1.refs_4_), channel_id=1, source_target_pairs={{0,2},{2,4},{4,6},{6,7},{7,5},{5,3},{3,1},{1,0},{8,10},{10,12},{12... | collective-permute-start | bytes 393224 | tf_op jit(solution)/shard_map/ppermute | solution.py:101
  79.6 18.0 %copy-start.5 = (bf16[128,512]{1,0:T(8,128)(2,1)}, bf16[128,512]{1,0:T(8,128)(2,1)S(1)}, u32[]{:S(2)}) copy-start(bf16[128,512]{1,0:T(8,128)(2,1)S(1)} %collective-permute-done.20.refs_18_) | copy-start | bytes 393220
  79.6 5.9 %collective-permute-start.21 = (bf16[128,512]{1,0:T(8,128)(2,1)S(1)}, bf16[128,512]{1,0:T(8,128)(2,1)S(1)}, u32[]{:S(2)}, u32[]{:S(2)}) collective-permute-start(bf16[128,512]{1,0:T(8,128)(2,1)S(1)} %collective-permute-done.20.refs_18_), channel_id=1, source_target_pairs={{0,1},{2,0},{4,2},{6,4},{7,6},{5,7},{3,5},{1,3},{8,9},{10,8},{12,1... | collective-permute-start | bytes 393224 | tf_op jit(solution)/shard_map/ppermute | solution.py:101
  82.4 15.2 %copy-start.6 = (bf16[128,512]{1,0:T(8,128)(2,1)}, bf16[128,512]{1,0:T(8,128)(2,1)S(1)}, u32[]{:S(2)}) copy-start(bf16[128,512]{1,0:T(8,128)(2,1)S(1)} %collective-permute-done.24.refs_17_) | copy-start | bytes 393220
  82.4 6.4 %collective-permute-start.25 = (bf16[128,512]{1,0:T(8,128)(2,1)S(1)}, bf16[128,512]{1,0:T(8,128)(2,1)S(1)}, u32[]{:S(2)}, u32[]{:S(2)}) collective-permute-start(bf16[128,512]{1,0:T(8,128)(2,1)S(1)} %collective-permute-done.24.refs_17_), channel_id=1, source_target_pairs={{0,1},{2,0},{4,2},{6,4},{7,6},{5,7},{3,5},{1,3},{8,9},{10,8},{12,1... | collective-permute-start | bytes 393224 | tf_op jit(solution)/shard_map/ppermute | solution.py:101
  84.2 13.5 %copy-start.7 = (bf16[128,512]{1,0:T(8,128)(2,1)}, bf16[128,512]{1,0:T(8,128)(2,1)S(1)}, u32[]{:S(2)}) copy-start(bf16[128,512]{1,0:T(8,128)(2,1)S(1)} %collective-permute-done.15.refs_7_) | copy-start | bytes 393220
  84.2 6.4 %collective-permute-start.17 = (bf16[128,512]{1,0:T(8,128)(2,1)S(1)}, bf16[128,512]{1,0:T(8,128)(2,1)S(1)}, u32[]{:S(2)}, u32[]{:S(2)}) collective-permute-start(bf16[128,512]{1,0:T(8,128)(2,1)S(1)} %collective-permute-done.15.refs_7_), channel_id=1, source_target_pairs={{0,2},{2,4},{4,6},{6,7},{7,5},{5,3},{3,1},{1,0},{8,10},{10,12},{12... | collective-permute-start | bytes 393224 | tf_op jit(solution)/shard_map/ppermute | solution.py:101
  84.5 13.2 %copy-start.8 = (bf16[128,512]{1,0:T(8,128)(2,1)}, bf16[128,512]{1,0:T(8,128)(2,1)S(1)}, u32[]{:S(2)}) copy-start(bf16[128,512]{1,0:T(8,128)(2,1)S(1)} %collective-permute-done.14.refs_6_) | copy-start | bytes 393220
  84.5 7.0 %collective-permute-start.16 = (bf16[128,512]{1,0:T(8,128)(2,1)S(1)}, bf16[128,512]{1,0:T(8,128)(2,1)S(1)}, u32[]{:S(2)}, u32[]{:S(2)}) collective-permute-start(bf16[128,512]{1,0:T(8,128)(2,1)S(1)} %collective-permute-done.14.refs_6_), channel_id=1, source_target_pairs={{0,2},{2,4},{4,6},{6,7},{7,5},{5,3},{3,1},{1,0},{8,10},{10,12},{12... | collective-permute-start | bytes 393224 | tf_op jit(solution)/shard_map/ppermute | solution.py:101
  85.5 12.1 %copy-start.9 = (bf16[128,512]{1,0:T(8,128)(2,1)}, bf16[128,512]{1,0:T(8,128)(2,1)S(1)}, u32[]{:S(2)}) copy-start(bf16[128,512]{1,0:T(8,128)(2,1)S(1)} %collective-permute-done.21.refs_16_) | copy-start | bytes 393220
  85.5 6.3 %collective-permute-start.22 = (bf16[128,512]{1,0:T(8,128)(2,1)S(1)}, bf16[128,512]{1,0:T(8,128)(2,1)S(1)}, u32[]{:S(2)}, u32[]{:S(2)}) collective-permute-start(bf16[128,512]{1,0:T(8,128)(2,1)S(1)} %collective-permute-done.21.refs_16_), channel_id=1, source_target_pairs={{0,1},{2,0},{4,2},{6,4},{7,6},{5,7},{3,5},{1,3},{8,9},{10,8},{12,1... | collective-permute-start | bytes 393224 | tf_op jit(solution)/shard_map/ppermute | solution.py:101
  88.8 8.9 %copy-start.10 = (bf16[128,512]{1,0:T(8,128)(2,1)}, bf16[128,512]{1,0:T(8,128)(2,1)S(1)}, u32[]{:S(2)}) copy-start(bf16[128,512]{1,0:T(8,128)(2,1)S(1)} %collective-permute-done.25.refs_15_) | copy-start | bytes 393220
  88.8 5.6 %collective-permute-start.26 = (bf16[128,512]{1,0:T(8,128)(2,1)S(1)}, bf16[128,512]{1,0:T(8,128)(2,1)S(1)}, u32[]{:S(2)}, u32[]{:S(2)}) collective-permute-start(bf16[128,512]{1,0:T(8,128)(2,1)S(1)} %collective-permute-done.25.refs_15_), channel_id=1, source_target_pairs={{0,1},{2,0},{4,2},{6,4},{7,6},{5,7},{3,5},{1,3},{8,9},{10,8},{12,1... | collective-permute-start | bytes 393224 | tf_op jit(solution)/shard_map/ppermute | solution.py:101
  90.5 7.2 %copy-start.11 = (bf16[128,512]{1,0:T(8,128)(2,1)}, bf16[128,512]{1,0:T(8,128)(2,1)S(1)}, u32[]{:S(2)}) copy-start(bf16[128,512]{1,0:T(8,128)(2,1)S(1)} %collective-permute-done.17.refs_9_) | copy-start | bytes 393220
  90.5 5.0 %collective-permute-start.19 = (bf16[128,512]{1,0:T(8,128)(2,1)S(1)}, bf16[128,512]{1,0:T(8,128)(2,1)S(1)}, u32[]{:S(2)}, u32[]{:S(2)}) collective-permute-start(bf16[128,512]{1,0:T(8,128)(2,1)S(1)} %collective-permute-done.17.refs_9_), channel_id=1, source_target_pairs={{0,2},{2,4},{4,6},{6,7},{7,5},{5,3},{3,1},{1,0},{8,10},{10,12},{12... | collective-permute-start | bytes 393224 | tf_op jit(solution)/shard_map/ppermute | solution.py:101
  91.5 6.2 %copy-start.12 = (bf16[128,512]{1,0:T(8,128)(2,1)}, bf16[128,512]{1,0:T(8,128)(2,1)S(1)}, u32[]{:S(2)}) copy-start(bf16[128,512]{1,0:T(8,128)(2,1)S(1)} %collective-permute-done.16.refs_8_) | copy-start | bytes 393220
  91.5 5.4 %collective-permute-start.18 = (bf16[128,512]{1,0:T(8,128)(2,1)S(1)}, bf16[128,512]{1,0:T(8,128)(2,1)S(1)}, u32[]{:S(2)}, u32[]{:S(2)}) collective-permute-start(bf16[128,512]{1,0:T(8,128)(2,1)S(1)} %collective-permute-done.16.refs_8_), channel_id=1, source_target_pairs={{0,2},{2,4},{4,6},{6,7},{7,5},{5,3},{3,1},{1,0},{8,10},{10,12},{12... | collective-permute-start | bytes 393224 | tf_op jit(solution)/shard_map/ppermute | solution.py:101
  91.8 5.1 %copy-start.13 = (bf16[128,512]{1,0:T(8,128)(2,1)}, bf16[128,512]{1,0:T(8,128)(2,1)S(1)}, u32[]{:S(2)}) copy-start(bf16[128,512]{1,0:T(8,128)(2,1)S(1)} %collective-permute-done.22.refs_14_) | copy-start | bytes 393220
  91.8 5.1 %collective-permute-start.23 = (bf16[128,512]{1,0:T(8,128)(2,1)S(1)}, bf16[128,512]{1,0:T(8,128)(2,1)S(1)}, u32[]{:S(2)}, u32[]{:S(2)}) collective-permute-start(bf16[128,512]{1,0:T(8,128)(2,1)S(1)} %collective-permute-done.22.refs_14_), channel_id=1, source_target_pairs={{0,1},{2,0},{4,2},{6,4},{7,6},{5,7},{3,5},{1,3},{8,9},{10,8},{12,1... | collective-permute-start | bytes 393224 | tf_op jit(solution)/shard_map/ppermute | solution.py:101
  94.4 2.5 %copy-start.14 = (bf16[128,512]{1,0:T(8,128)(2,1)}, bf16[128,512]{1,0:T(8,128)(2,1)S(1)}, u32[]{:S(2)}) copy-start(bf16[128,512]{1,0:T(8,128)(2,1)S(1)} %collective-permute-done.26.refs_13_) | copy-start | bytes 393220
  95.5 1.4 %copy-start.15 = (bf16[128,512]{1,0:T(8,128)(2,1)}, bf16[128,512]{1,0:T(8,128)(2,1)S(1)}, u32[]{:S(2)}) copy-start(bf16[128,512]{1,0:T(8,128)(2,1)S(1)} %collective-permute-done.19.refs_11_) | copy-start | bytes 393220
  96.9 0.6 copy-start.16
  96.9 0.7 copy-start.17
where the time goes:
time: 102 us
  waiting for transfers between devices  39.1 us (38%)
  starting transfers between devices  30.4 us (30%)
  matrix products  18.2 us (18%)
  local copies, waits for them, and re-layouts  6.55 us (6%)
  Pallas kernels  4 us (4%)
  other arithmetic  2.06 us (2%)
  between operations  1.43 us (1%)
    ppermute x21, starting transfers between devices, shift_in_ring(): return lax.ppermute(value, 'tensor', pairs)  20.8 us
    ppermute x21, waiting for transfers between devices, shift_in_ring(): return lax.ppermute(value, 'tensor', pairs)  19.8 us
    ppermute x2, waiting for transfers between devices, shift_pairs(): lax.ppermute(value, 'dp', [(i, (i + 2) % count) for i in range(count)])  15.2 us
    dot_general x4, matrix products, exchanged_body(): jnp.dot(part, shard, preferred_element_type=jnp.float32)  6.15 us
    all_to_all x1, starting transfers between devices, exchanged_body(): column_weight = lax.all_to_all(output_weight, 'tensor', 1, 0, tiled=True)  5.81 us
    dot_general x4, matrix products, exchanged_body(): summed = jnp.dot(gathered, shard, preferred_element_type=jnp.float32)  5.67 us
    all_to_all x1, waiting for transfers between devices, exchanged_body(): column_weight = lax.all_to_all(output_weight, 'tensor', 1, 0, tiled=True)  4.14 us
    pallas_call x1, Pallas kernels, finish(): pl.pallas_call(lambda *refs: finish_kernel(*refs, width=width), out_shape...  4 us
  transfers between devices with their start and end apart: 28, of which 14 were waited for; matrix products, arithmetic and copies ran while one was open for 25% of the time, Pallas kernels for 0%

commit v1 on v0

--- a/solution.py
+++ b/solution.py
@@ -145,15 +145,15 @@
     return found
 
 
-def finish_kernel(own_t, own_d, gain, *refs, width):
+def finish_kernel(own_t, own_d, gain, early, *refs, counted, width):
     chunks, (hidden, normed) = refs[:-2], refs[-2:]
     features = normed.shape[1]
     squares = jnp.zeros((normed.shape[0], 128), jnp.float32)
-    for chunk in chunks:
-        for i in range(chunk.shape[1] // 128):
+    for k, chunk in enumerate(chunks):
+        for i in range(0 if k in counted else chunk.shape[1] // 128):
             part = chunk[:, i * 128 : (i + 1) * 128].astype(jnp.float32)
             squares = squares + part * part
-    scale = lax.rsqrt(jnp.sum(squares, axis=1, keepdims=True) / features + norm_eps)
+    scale = lax.rsqrt((jnp.sum(squares, axis=1, keepdims=True) + early[...]) / features + norm_eps)
     own_rows = pl.ds(pl.multiple_of(own_t[0] * hidden.shape[0], hidden.shape[0]), hidden.shape[0])
     per_chunk = chunks[0].shape[1] // width
     count_t = len(chunks) // 2
@@ -171,24 +171,25 @@
             hidden[:, columns] = chunk[own_rows, i * width : (i + 1) * width]
 
 
-def finish(chunks, own_count, norm_gain, width):
+def finish(chunks, squares, counted, own_count, norm_gain, width):
     rows = chunks[0].shape[0]
     features = norm_gain.shape[0]
     smem = pl.BlockSpec(memory_space=pltpu.SMEM)
     vmem = pl.BlockSpec(memory_space=pltpu.VMEM)
     return pl.pallas_call(
-        lambda *refs: finish_kernel(*refs, width=width),
+        lambda *refs: finish_kernel(*refs, counted=counted, width=width),
         out_shape=(
             jax.ShapeDtypeStruct((own_count, features), jnp.bfloat16),
             jax.ShapeDtypeStruct((rows, features), jnp.bfloat16),
         ),
-        in_specs=[smem, smem] + [vmem] * (1 + len(chunks)),
+        in_specs=[smem, smem] + [vmem] * (2 + len(chunks)),
         out_specs=(vmem, vmem),
         name="finish",
     )(
         lax.axis_index("tensor").reshape(1),
         lax.axis_index("dp").reshape(1),
         norm_gain.reshape(1, features),
+        squares,
         *chunks,
     )
 
@@ -239,9 +240,14 @@
     count = len(blocks) // 2
     parts = [jnp.concatenate(blocks[i * count : (i + 1) * count], axis=1) for i in range(2)]
     near = ring_gather(parts[0], 1)
+    early = (1, count_t - 1) if count_t > 2 else ()
+    squares = sum(
+        [jnp.sum(jnp.square(near[k].astype(jnp.float32)), axis=-1, keepdims=True) for k in early],
+        jnp.zeros((tok_count, 1), jnp.float32),
+    )
     far = ring_gather(parts[1], -1)
     chunks = [chunk for got in zip(near, far) for chunk in got]
-    return finish(chunks, tok_count // count_t, norm_gain, width)
+    return finish(chunks, squares, [2 * k for k in early], tok_count // count_t, norm_gain, width)
 
 
 def body(*arrays):

time: 102 us -> 102 us (level)
    unnamed x41 -> x31, local copies, waits for them, and re-layouts: 3.98 us -> 3.29 us
  transfers between devices with their start and end apart: 28 -> 28, of which waited for: 14 -> 15; matrix products, arithmetic and copies ran while one was open for 25% -> 26% of each run, Pallas kernels for 0% -> 0%
where the time goes in v1:
time: 102 us; the launch traced here: 101 us
  waiting for transfers between devices  38.4 us (38%)
  starting transfers between devices  30.4 us (30%)
  matrix products  18.2 us (18%)
  local copies, waits for them, and re-layouts  6.6 us (6%)
  Pallas kernels  4.06 us (4%)
  other arithmetic  2.3 us (2%)
  between operations  1.41 us (1%)
    ppermute x21, starting transfers between devices, shift_in_ring(): return lax.ppermute(value, 'tensor', pairs)  20.8 us
    ppermute x21, waiting for transfers between devices, shift_in_ring(): return lax.ppermute(value, 'tensor', pairs)  19 us
    ppermute x2, waiting for transfers between devices, shift_pairs(): lax.ppermute(value, 'dp', [(i, (i + 2) % count) for i in range(count)])  15.2 us
    dot_general x4, matrix products, exchanged_body(): jnp.dot(part, shard, preferred_element_type=jnp.float32)  6.14 us
    all_to_all x1, starting transfers between devices, exchanged_body(): column_weight = lax.all_to_all(output_weight, 'tensor', 1, 0, tiled=True)  5.81 us
    dot_general x4, matrix products, exchanged_body(): summed = jnp.dot(gathered, shard, preferred_element_type=jnp.float32)  5.67 us
    all_to_all x1, waiting for transfers between devices, exchanged_body(): column_weight = lax.all_to_all(output_weight, 'tensor', 1, 0, tiled=True)  4.13 us
    pallas_call x1, Pallas kernels, finish(): pl.pallas_call(lambda *refs: finish_kernel(*refs, counted=counted, width=...  4.06 us
  transfers between devices with their start and end apart: 28, of which 15 were waited for; matrix products, arithmetic and copies ran while one was open for 26% of the time, Pallas kernels for 0%

profile of v1, /device:TPU:0, one launch (start us, length us, event | category | flops | bytes accessed | tf_op | source)
XLA Modules:
  0.0 101.3 jit_solution(4987571625140425124)
XLA Ops:
  0.7 3.1 %collective-permute-start.1 = (bf16[2048,256]{1,0:T(8,128)(2,1)}, bf16[2048,256]{1,0:T(8,128)(2,1)}, u32[]{:S(2)}, u32[]{:S(2)}) collective-permute-start(bf16[2048,256]{1,0:T(8,128)(2,1)} %param.10), channel_id=1, source_target_pairs={{0,16},{8,24},{16,0},{24,8},{1,17},{9,25},{17,1},{25,9},{2,18},{10... | collective-permute-start | bytes 3145736 | tf_op jit(solution)/shard_map/ppermute | solution.py:133
  3.7 2.3 %copy.21 = bf16[256,2048]{0,1:T(8,128)(2,1)} copy(bf16[256,2048]{1,0:T(8,128)(2,1)} %param.12) | data formatting | bytes 2097152 | tf_op args[4]
  6.0 5.8 %all-to-all-start = ((bf16[256,8,256]{0,2,1:T(8,128)(2,1)}), bf16[256,8,256]{0,2,1:T(8,128)(2,1)S(1)}, u32[]{:S(2)}, u32[]{:S(2)}) async-start(bf16[256,8,256]{0,2,1:T(8,128)(2,1)} %bitcast.47), calls=%async_computation | async-start | bytes 2097152 | tf_op jit(solution)/shard_map/all_to_all | solution.py:217
  11.8 0.1 iota_compare_fusion
  12.0 15.2 %collective-permute-done.1 = bf16[2048,256]{1,0:T(8,128)(2,1)} collective-permute-done((bf16[2048,256]{1,0:T(8,128)(2,1)}, bf16[2048,256]{1,0:T(8,128)(2,1)}, u32[]{:S(2)}, u32[]{:S(2)}) %collective-permute-start.1) | collective-permute-done | bytes 1048608 | tf_op jit(solution)/shard_map/ppermute | solution.py:133
  27.6 1.0 multiply_cosine_fusion
  28.6 1.5 %convolution_add_fusion.6 = f32[128,256]{1,0:T(8,128)S(1)} fusion(bf16[2048,256]{1,0:T(8,128)(2,1)} %param.10, bf16[128,8192]{1,0:T(8,128)(2,1)S(1)} %copy-done, s32[]{:T(128)S(6)} %select_n.152, f32[256]{0:T(256)S(1)} %convert_element_type.44), kind=kOutput, calls=%fused_computation.13 | convolution fusion | flops 134250496 | bytes 1704964 | tf_op jit(solution)/shard_map/dot_general | solution.py:222
  30.1 1.5 %fusion.11 = f32[128,256]{1,0:T(8,128)S(1)} fusion(bf16[2048,256]{1,0:T(8,128)(2,1)} %collective-permute-done.1, bf16[128,8192]{1,0:T(8,128)(2,1)S(1)} %copy-done, s32[]{:T(128)S(6)} %select_n.156), kind=kOutput, calls=%fused_computation.21 | convolution fusion | flops 134217728 | bytes 1703940 | tf_op jit(solution)/shard_map/dot_general | solution.py:222
  31.7 1.5 %fusion.5 = f32[128,256]{1,0:T(8,128)S(1)} fusion(f32[128,256]{1,0:T(8,128)S(1)} %fusion.11, f32[128,256]{1,0:T(8,128)S(1)} %convolution_add_fusion.6, bf16[2048,256]{1,0:T(8,128)(2,1)} %collective-permute-done, bf16[128,8192]{1,0:T(8,128)(2,1)S(1)} %copy-done, s32[]{:T(128)S(6)} %select_n.154), kind=kOutput, calls=%fused_computation.12 | convolution fusion | flops 134283264 | bytes 1966084 | tf_op jit(solution)/shard_map/dot_general | solution.py:222
  33.3 4.1 %all-to-all-done = bf16[256,8,256]{0,2,1:T(8,128)(2,1)S(1)} async-done(((bf16[256,8,256]{0,2,1:T(8,128)(2,1)}), bf16[256,8,256]{0,2,1:T(8,128)(2,1)S(1)}, u32[]{:S(2)}, u32[]{:S(2)}) %all-to-all-start) | async-done | bytes 1048608 | tf_op jit(solution)/shard_map/all_to_all | solution.py:217
  37.4 1.0 copy-done.1
  38.4 1.5 %copy.22 = bf16[8,256,256]{2,1,0:T(8,128)(2,1)S(1)} copy(bf16[8,256,256]{1,2,0:T(8,128)(2,1)} %bitcast.46) | data formatting | bytes 2097152 | tf_op jit(solution)/shard_map/all_to_all | solution.py:217
  39.8 0.6 collective-permute-start.13
  40.4 1.5 %convolution_add_fusion.4 = f32[128,256]{1,0:T(8,128)S(1)} fusion(f32[128,256]{1,0:T(8,128)S(1)} %fusion.5, bf16[2048,256]{1,0:T(8,128)(2,1)} %collective-permute-done.2, bf16[128,8192]{1,0:T(8,128)(2,1)S(1)} %copy-done, s32[]{:T(128)S(6)} %select_n.158), kind=kOutput, calls=%fused_computation.10 | convolution fusion | flops 134250496 | bytes 1835012 | tf_op jit(solution)/shard_map/dot_general | solution.py:222
  42.0 0.1 reshape.120
  42.1 0.2 fusion.29
  42.3 0.9 subtract_convert_fusion
  43.2 2.3 %fusion.4 = f32[2,128,1024]{2,1,0:T(8,128)} fusion(pred[128,1024]{1,0:T(8,128)(4,1)S(1)} %iota_compare_fusion, bf16[1,1,1024,128]{3,2,1,0:T(8,128)(2,1)} %param.13, bf16[128,2,64]{2,0,1:T(8,128)(2,1)S(1)} %get-tuple-element.3, bf16[128,2,64]{2,0,1:T(8,128)(2,1)S(1)} %get-tuple-element.2), kind=kOutput, calls=%fused_computation.5 | convolution fusion | flops 67764224 | bytes 1507328 | tf_op jit(solution)/shard_map/thd,kd->htk/dot_general | solution.py:34
  45.5 1.6 %fusion.30 = f32[2,128]{1,0:T(2,128)S(1)} fusion(pred[128,1024]{1,0:T(8,128)(4,1)S(1)} %iota_compare_fusion, bf16[1,1,1024,128]{3,2,1,0:T(8,128)(2,1)} %param.13, bf16[128,2,64]{2,0,1:T(8,128)(2,1)S(1)} %get-tuple-element.3, bf16[128,2,64]{2,0,1:T(8,128)(2,1)S(1)} %get-tuple-element.2), kind=kOutput, calls=%fused_computation.59 | convolution fusion | flops 68289536 | bytes 459776 | tf_op jit(solution)/shard_map/sub | solution.py:40
  47.1 2.5 %convolution_convert_fusion = bf16[2,128,128]{1,2,0:T(8,128)(2,1)S(1)} fusion(f32[2,128]{1,0:T(2,128)S(1)} %fusion.30, bf16[1,1,1024,128]{3,2,1,0:T(8,128)(2,1)} %param.14, f32[2,128,1024]{2,1,0:T(8,128)} %fusion.4), kind=kOutput, calls=%fused_computation.18 | convolution fusion | flops 67929344 | bytes 1377280 | tf_op jit(solution)/shard_map/htk,kd->thd/dot_general | solution.py:42
  49.6 2.0 %collective-permute-start.7 = (bf16[128,256]{0,1:T(8,128)(2,1)S(1)}, bf16[128,256]{0,1:T(8,128)(2,1)S(1)}, u32[]{:S(2)}, u32[]{:S(2)}) collective-permute-start(bf16[128,256]{0,1:T(8,128)(2,1)S(1)} %bitcast.49), channel_id=1, source_target_pairs={{0,1},{2,0},{4,2},{6,4},{7,6},{5,7},{3,5},{1,3},{8,9},{10,8},{12,1... | collective-permute-start | bytes 196616 | tf_op jit(solution)/shard_map/ppermute | solution.py:101
  51.6 0.1 broadcast_in_dim.10
  51.7 2.4 %collective-permute-done.3 = bf16[128,256]{0,1:T(8,128)(2,1)S(1)} collective-permute-done((bf16[128,256]{0,1:T(8,128)(2,1)S(1)}, bf16[128,256]{0,1:T(8,128)(2,1)S(1)}, u32[]{:S(2)}, u32[]{:S(2)}) %collective-permute-start.3) | collective-permute-done | bytes 65568 | tf_op jit(solution)/shard_map/ppermute | solution.py:101
  54.1 0.3 collective-permute-start.4
  54.4 1.7 %collective-permute-start.8 = (bf16[128,256]{0,1:T(8,128)(2,1)S(1)}, bf16[128,256]{0,1:T(8,128)(2,1)S(1)}, u32[]{:S(2)}, u32[]{:S(2)}) collective-permute-start(bf16[128,256]{0,1:T(8,128)(2,1)S(1)} %collective-permute-done.7), channel_id=1, source_target_pairs={{0,1},{2,0},{4,2},{6,4},{7,6},{5,7},{3,5},{1,3},{8,9},{10,8},{12,1... | collective-permute-start | bytes 196616 | tf_op jit(solution)/shard_map/ppermute | solution.py:101
  56.1 2.2 %collective-permute-done.4 = bf16[128,256]{0,1:T(8,128)(2,1)S(1)} collective-permute-done((bf16[128,256]{0,1:T(8,128)(2,1)S(1)}, bf16[128,256]{0,1:T(8,128)(2,1)S(1)}, u32[]{:S(2)}, u32[]{:S(2)}) %collective-permute-start.4) | collective-permute-done | bytes 65568 | tf_op jit(solution)/shard_map/ppermute | solution.py:101
  58.3 0.3 collective-permute-start.5
  58.6 1.7 %collective-permute-start.9 = (bf16[128,256]{0,1:T(8,128)(2,1)S(1)}, bf16[128,256]{0,1:T(8,128)(2,1)S(1)}, u32[]{:S(2)}, u32[]{:S(2)}) collective-permute-start(bf16[128,256]{0,1:T(8,128)(2,1)S(1)} %collective-permute-done.8), channel_id=1, source_target_pairs={{0,1},{2,0},{4,2},{6,4},{7,6},{5,7},{3,5},{1,3},{8,9},{10,8},{12,1... | collective-permute-start | bytes 196616 | tf_op jit(solution)/shard_map/ppermute | solution.py:101
  60.4 2.2 %collective-permute-done.5 = bf16[128,256]{0,1:T(8,128)(2,1)S(1)} collective-permute-done((bf16[128,256]{0,1:T(8,128)(2,1)S(1)}, bf16[128,256]{0,1:T(8,128)(2,1)S(1)}, u32[]{:S(2)}, u32[]{:S(2)}) %collective-permute-start.5) | collective-permute-done | bytes 65568 | tf_op jit(solution)/shard_map/ppermute | solution.py:101
  62.6 0.3 collective-permute-start.6
  62.9 4.0 %collective-permute-done.6 = bf16[128,256]{0,1:T(8,128)(2,1)S(1)} collective-permute-done((bf16[128,256]{0,1:T(8,128)(2,1)S(1)}, bf16[128,256]{0,1:T(8,128)(2,1)S(1)}, u32[]{:S(2)}, u32[]{:S(2)}) %collective-permute-start.6) | collective-permute-done | bytes 65568 | tf_op jit(solution)/shard_map/ppermute | solution.py:101
  66.9 0.1 collective-permute-start.14
  67.1 1.2 %fusion.6 = bf16[128,256]{1,0:T(8,128)(2,1)S(1)} fusion(bf16[128,2048]{0,1:T(8,128)(2,1)S(1)} %constant_dynamic-update-slice_fusion, bf16[2048,256]{1,0:T(8,128)(2,1)S(1)} %bitcast.45, bf16[128,8192]{1,0:T(8,128)(2,1)} %param.9, s32[]{:T(128)S(6)} %select_n.151), kind=kOutput, calls=%fused_computation.14 | convolution fusion | flops 134316032 | bytes 1703940 | tf_op jit(solution)/shard_map/dot_general | solution.py:236
  68.3 1.6 %fusion.7 = bf16[128,256]{1,0:T(8,128)(2,1)S(1)} fusion(bf16[128,2048]{0,1:T(8,128)(2,1)S(1)} %constant_dynamic-update-slice_fusion, bf16[2048,256]{1,0:T(8,128)(2,1)} %collective-permute-done.10, bf16[128,8192]{1,0:T(8,128)(2,1)} %param.9, s32[]{:T(128)S(6)} %select_n.188), kind=kOutput, calls=%fused_computation.15 | convolution fusion | flops 134316032 | bytes 1703940 | tf_op jit(solution)/shard_map/dot_general | solution.py:236
  70.0 0.3 collective-permute-start.11
  70.3 1.6 %fusion.8 = bf16[128,256]{1,0:T(8,128)(2,1)S(1)} fusion(bf16[128,2048]{0,1:T(8,128)(2,1)S(1)} %constant_dynamic-update-slice_fusion, bf16[2048,256]{1,0:T(8,128)(2,1)} %collective-permute-done.13, bf16[128,8192]{1,0:T(8,128)(2,1)} %param.9, s32[]{:T(128)S(6)} %select_n.189), kind=kOutput, calls=%fused_computation.16 | convolution fusion | flops 134316032 | bytes 1703940 | tf_op jit(solution)/shard_map/dot_general | solution.py:236
  71.9 1.2 %fusion.9 = bf16[128,256]{1,0:T(8,128)(2,1)S(1)} fusion(bf16[128,2048]{0,1:T(8,128)(2,1)S(1)} %constant_dynamic-update-slice_fusion, bf16[2048,256]{1,0:T(8,128)(2,1)S(1)} %collective-permute-done.14, bf16[128,8192]{1,0:T(8,128)(2,1)} %param.9, s32[]{:T(128)S(6)} %select_n.190), kind=kOutput, calls=%fused_computation.17 | convolution fusion | flops 134316032 | bytes 1703940 | tf_op jit(solution)/shard_map/dot_general | solution.py:236
  73.2 1.8 %collective-permute-start.21 = (bf16[128,512]{1,0:T(8,128)(2,1)S(1)}, bf16[128,512]{1,0:T(8,128)(2,1)S(1)}, u32[]{:S(2)}, u32[]{:S(2)}) collective-permute-start(bf16[128,512]{1,0:T(8,128)(2,1)S(1)} %pad_maximum_fusion.1.refs_5_), channel_id=1, source_target_pairs={{0,1},{2,0},{4,2},{6,4},{7,6},{5,7},{3,5},{1,3},{8,9},{10,8},{12,1... | collective-permute-start | bytes 393224 | tf_op jit(solution)/shard_map/ppermute | solution.py:101
  75.0 1.3 %collective-permute-start.12 = (bf16[128,512]{1,0:T(8,128)(2,1)S(1)}, bf16[128,512]{1,0:T(8,128)(2,1)S(1)}, u32[]{:S(2)}, u32[]{:S(2)}) collective-permute-start(bf16[128,512]{1,0:T(8,128)(2,1)S(1)} %pad_maximum_fusion.refs_4_), channel_id=1, source_target_pairs={{0,1},{2,0},{4,2},{6,4},{7,6},{5,7},{3,5},{1,3},{8,9},{10,8},{12,1... | collective-permute-start | bytes 393224 | tf_op jit(solution)/shard_map/ppermute | solution.py:101
  76.3 0.7 collective-permute-start.16
  77.0 0.3 collective-permute-start.15
  77.3 2.3 %collective-permute-done.21.refs_19_ = bf16[128,512]{1,0:T(8,128)(2,1)S(1)} collective-permute-done((bf16[128,512]{1,0:T(8,128)(2,1)S(1)}, bf16[128,512]{1,0:T(8,128)(2,1)S(1)}, u32[]{:S(2)}, u32[]{:S(2)}) %collective-permute-start.21) | collective-permute-done | bytes 131104 | tf_op jit(solution)/shard_map/ppermute | solution.py:101
  79.6 1.7 %collective-permute-start.22 = (bf16[128,512]{1,0:T(8,128)(2,1)S(1)}, bf16[128,512]{1,0:T(8,128)(2,1)S(1)}, u32[]{:S(2)}, u32[]{:S(2)}) collective-permute-start(bf16[128,512]{1,0:T(8,128)(2,1)S(1)} %collective-permute-done.21.refs_19_), channel_id=1, source_target_pairs={{0,1},{2,0},{4,2},{6,4},{7,6},{5,7},{3,5},{1,3},{8,9},{10,8},{12,1... | collective-permute-start | bytes 393224 | tf_op jit(solution)/shard_map/ppermute | solution.py:101
  81.4 0.6 reshape.119.refs_2_
  82.0 0.4 collective-permute-done.12.refs_18_
  82.4 1.7 %collective-permute-start.25 = (bf16[128,512]{1,0:T(8,128)(2,1)S(1)}, bf16[128,512]{1,0:T(8,128)(2,1)S(1)}, u32[]{:S(2)}, u32[]{:S(2)}) collective-permute-start(bf16[128,512]{1,0:T(8,128)(2,1)S(1)} %collective-permute-done.12.refs_18_), channel_id=1, source_target_pairs={{0,1},{2,0},{4,2},{6,4},{7,6},{5,7},{3,5},{1,3},{8,9},{10,8},{12,1... | collective-permute-start | bytes 393224 | tf_op jit(solution)/shard_map/ppermute | solution.py:101
  84.2 0.3 collective-permute-start.18
  84.5 0.4 collective-permute-start.17
  84.9 0.7 collective-permute-done.22.refs_17_
  85.5 1.8 %collective-permute-start.23 = (bf16[128,512]{1,0:T(8,128)(2,1)S(1)}, bf16[128,512]{1,0:T(8,128)(2,1)}, u32[]{:S(2)}, u32[]{:S(2)}) collective-permute-start(bf16[128,512]{1,0:T(8,128)(2,1)S(1)} %collective-permute-done.22.refs_17_), channel_id=1, source_target_pairs={{0,1},{2,0},{4,2},{6,4},{7,6},{5,7},{3,5},{1,3},{8,9},{10,8},{12,1... | collective-permute-start | bytes 393224 | tf_op jit(solution)/shard_map/ppermute | solution.py:101
  87.3 0.1 multiply_reduce_fusion
  87.4 0.1 multiply_reduce_fusion.1
  87.5 1.3 %collective-permute-done.25.refs_16_ = bf16[128,512]{1,0:T(8,128)(2,1)S(1)} collective-permute-done((bf16[128,512]{1,0:T(8,128)(2,1)S(1)}, bf16[128,512]{1,0:T(8,128)(2,1)S(1)}, u32[]{:S(2)}, u32[]{:S(2)}) %collective-permute-start.25) | collective-permute-done | bytes 131104 | tf_op jit(solution)/shard_map/ppermute | solution.py:101
  88.8 1.7 %collective-permute-start.26 = (bf16[128,512]{1,0:T(8,128)(2,1)S(1)}, bf16[128,512]{1,0:T(8,128)(2,1)}, u32[]{:S(2)}, u32[]{:S(2)}) collective-permute-start(bf16[128,512]{1,0:T(8,128)(2,1)S(1)} %collective-permute-done.25.refs_16_), channel_id=1, source_target_pairs={{0,1},{2,0},{4,2},{6,4},{7,6},{5,7},{3,5},{1,3},{8,9},{10,8},{12,1... | collective-permute-start | bytes 393224 | tf_op jit(solution)/shard_map/ppermute | solution.py:101
  90.5 0.3 collective-permute-start.20
  90.8 0.7 collective-permute-done.17.refs_9_
  91.5 0.3 collective-permute-start.19
  91.8 1.7 %collective-permute-start.24 = (bf16[128,512]{1,0:T(8,128)(2,1)}, bf16[128,512]{1,0:T(8,128)(2,1)}, u32[]{:S(2)}, u32[]{:S(2)}) collective-permute-start(bf16[128,512]{1,0:T(8,128)(2,1)} %collective-permute-done.23.refs_15_), channel_id=1, source_target_pairs={{0,1},{2,0},{4,2},{6,4},{7,6},{5,7},{3,5},{1,3},{8,9},{10,8},{12,1... | collective-permute-start | bytes 393224 | tf_op jit(solution)/shard_map/ppermute | solution.py:101
  93.5 0.7 copy.23.refs_3_
  94.3 0.4 collective-permute-done.26.refs_14_
  94.6 1.0 collective-permute-done.20.refs_12_
  95.6 1.4 %collective-permute-done.19.refs_11_ = bf16[128,512]{1,0:T(8,128)(2,1)} collective-permute-done((bf16[128,512]{1,0:T(8,128)(2,1)S(1)}, bf16[128,512]{1,0:T(8,128)(2,1)}, u32[]{:S(2)}, u32[]{:S(2)}) %collective-permute-start.19) | collective-permute-done | bytes 131104 | tf_op jit(solution)/shard_map/ppermute | solution.py:101
  97.0 0.1 collective-permute-done.24.refs_13_
  97.2 4.1 %finish.1 = (bf16[16,8192]{1,0:T(8,128)(2,1)}, bf16[128,8192]{1,0:T(8,128)(2,1)}) custom-call(s32[1]{0:T(128)} %bitcast.refs_0_, s32[1]{0:T(128)} %bitcast.1.refs_1_, bf16[1,8192]{1,0:T(2,128)(2,1)} %reshape.119.refs_2_, f32[128,1]{1,0:T(8,128)} %copy.23.refs_3_, bf16[128,512]{1,0:T(8,128)(2,1)} %copy-done.2, bf16[128,512]{1,0:T(8,128)(2,1)} %copy-done.4, ...), custom_call_target="tpu_custom_call" | custom-call | tf_op jit(solution)/shard_map/finish/pallas_call | solution.py:179
  (61 shorter events, 0.3 us)
Async XLA Ops:
  0.6 28.0 %copy-start = (bf16[128,8192]{1,0:T(8,128)(2,1)S(1)}, bf16[128,8192]{1,0:T(8,128)(2,1)}, u32[]{:S(2)}) copy-start(bf16[128,8192]{1,0:T(8,128)(2,1)} %param.8) | copy-start | bytes 6291460
  0.6 26.9 %copy-start.14 = (bf16[256]{0:T(256)(128)(2,1)S(1)}, bf16[256]{0:T(256)(128)(2,1)}, u32[]{:S(2)}) copy-start(bf16[256]{0:T(256)(128)(2,1)} %param.11) | copy-start | bytes 1540
  0.7 26.5 %collective-permute-start.1 = (bf16[2048,256]{1,0:T(8,128)(2,1)}, bf16[2048,256]{1,0:T(8,128)(2,1)}, u32[]{:S(2)}, u32[]{:S(2)}) collective-permute-start(bf16[2048,256]{1,0:T(8,128)(2,1)} %param.10), channel_id=1, source_target_pairs={{0,16},{8,24},{16,0},{24,8},{1,17},{9,25},{17,1},{25,9},{2,18},{10... | collective-permute-start | bytes 3145736 | tf_op jit(solution)/shard_map/ppermute | solution.py:133
  6.0 31.4 %all-to-all-start = ((bf16[256,8,256]{0,2,1:T(8,128)(2,1)}), bf16[256,8,256]{0,2,1:T(8,128)(2,1)S(1)}, u32[]{:S(2)}, u32[]{:S(2)}) async-start(bf16[256,8,256]{0,2,1:T(8,128)(2,1)} %bitcast.47), calls=%async_computation | async-start | bytes 2097152 | tf_op jit(solution)/shard_map/all_to_all | solution.py:217
  11.8 19.9 %collective-permute-start = (bf16[2048,256]{1,0:T(8,128)(2,1)}, bf16[2048,256]{1,0:T(8,128)(2,1)}, u32[]{:S(2)}, u32[]{:S(2)}) collective-permute-start(bf16[2048,256]{1,0:T(8,128)(2,1)} %param.10), channel_id=1, source_target_pairs={{0,8},{8,0},{16,24},{24,16},{1,9},{9,1},{17,25},{25,17},{2,10},{10... | collective-permute-start | bytes 3145736 | tf_op jit(solution)/shard_map/ppermute | solution.py:128
  27.2 13.2 %collective-permute-start.2 = (bf16[2048,256]{1,0:T(8,128)(2,1)}, bf16[2048,256]{1,0:T(8,128)(2,1)}, u32[]{:S(2)}, u32[]{:S(2)}) collective-permute-start(bf16[2048,256]{1,0:T(8,128)(2,1)} %collective-permute-done.1), channel_id=1, source_target_pairs={{0,8},{8,0},{16,24},{24,16},{1,9},{9,1},{17,25},{25,17},{2,10},{10... | collective-permute-start | bytes 3145736 | tf_op jit(solution)/shard_map/ppermute | solution.py:128
  37.4 1.0 copy-start.1
  39.8 27.1 %collective-permute-start.13 = (bf16[2048,256]{1,0:T(8,128)(2,1)S(1)}, bf16[2048,256]{1,0:T(8,128)(2,1)}, u32[]{:S(2)}, u32[]{:S(2)}) collective-permute-start(bf16[2048,256]{1,0:T(8,128)(2,1)S(1)} %bitcast.43), channel_id=1, source_target_pairs={{0,16},{8,24},{16,0},{24,8},{1,17},{9,25},{17,1},{25,9},{2,18},{10... | collective-permute-start | bytes 3145736 | tf_op jit(solution)/shard_map/ppermute | solution.py:133
  40.4 27.9 %collective-permute-start.10 = (bf16[2048,256]{1,0:T(8,128)(2,1)S(1)}, bf16[2048,256]{1,0:T(8,128)(2,1)}, u32[]{:S(2)}, u32[]{:S(2)}) collective-permute-start(bf16[2048,256]{1,0:T(8,128)(2,1)S(1)} %bitcast.44), channel_id=1, source_target_pairs={{0,8},{8,0},{16,24},{24,16},{1,9},{9,1},{17,25},{25,17},{2,10},{10... | collective-permute-start | bytes 3145736 | tf_op jit(solution)/shard_map/ppermute | solution.py:128
  49.5 4.6 %collective-permute-start.3 = (bf16[128,256]{0,1:T(8,128)(2,1)S(1)}, bf16[128,256]{0,1:T(8,128)(2,1)S(1)}, u32[]{:S(2)}, u32[]{:S(2)}) collective-permute-start(bf16[128,256]{0,1:T(8,128)(2,1)S(1)} %bitcast.48), channel_id=1, source_target_pairs={{0,2},{2,4},{4,6},{6,7},{7,5},{5,3},{3,1},{1,0},{8,10},{10,12},{12... | collective-permute-start | bytes 196616 | tf_op jit(solution)/shard_map/ppermute | solution.py:101
  49.6 4.8 %collective-permute-start.7 = (bf16[128,256]{0,1:T(8,128)(2,1)S(1)}, bf16[128,256]{0,1:T(8,128)(2,1)S(1)}, u32[]{:S(2)}, u32[]{:S(2)}) collective-permute-start(bf16[128,256]{0,1:T(8,128)(2,1)S(1)} %bitcast.49), channel_id=1, source_target_pairs={{0,1},{2,0},{4,2},{6,4},{7,6},{5,7},{3,5},{1,3},{8,9},{10,8},{12,1... | collective-permute-start | bytes 196616 | tf_op jit(solution)/shard_map/ppermute | solution.py:101
  54.1 4.3 %collective-permute-start.4 = (bf16[128,256]{0,1:T(8,128)(2,1)S(1)}, bf16[128,256]{0,1:T(8,128)(2,1)S(1)}, u32[]{:S(2)}, u32[]{:S(2)}) collective-permute-start(bf16[128,256]{0,1:T(8,128)(2,1)S(1)} %collective-permute-done.3), channel_id=1, source_target_pairs={{0,2},{2,4},{4,6},{6,7},{7,5},{5,3},{3,1},{1,0},{8,10},{10,12},{12... | collective-permute-start | bytes 196616 | tf_op jit(solution)/shard_map/ppermute | solution.py:101
  54.4 4.3 %collective-permute-start.8 = (bf16[128,256]{0,1:T(8,128)(2,1)S(1)}, bf16[128,256]{0,1:T(8,128)(2,1)S(1)}, u32[]{:S(2)}, u32[]{:S(2)}) collective-permute-start(bf16[128,256]{0,1:T(8,128)(2,1)S(1)} %collective-permute-done.7), channel_id=1, source_target_pairs={{0,1},{2,0},{4,2},{6,4},{7,6},{5,7},{3,5},{1,3},{8,9},{10,8},{12,1... | collective-permute-start | bytes 196616 | tf_op jit(solution)/shard_map/ppermute | solution.py:101
  58.3 4.3 %collective-permute-start.5 = (bf16[128,256]{0,1:T(8,128)(2,1)S(1)}, bf16[128,256]{0,1:T(8,128)(2,1)S(1)}, u32[]{:S(2)}, u32[]{:S(2)}) collective-permute-start(bf16[128,256]{0,1:T(8,128)(2,1)S(1)} %collective-permute-done.4), channel_id=1, source_target_pairs={{0,2},{2,4},{4,6},{6,7},{7,5},{5,3},{3,1},{1,0},{8,10},{10,12},{12... | collective-permute-start | bytes 196616 | tf_op jit(solution)/shard_map/ppermute | solution.py:101
  58.6 8.3 %collective-permute-start.9 = (bf16[128,256]{0,1:T(8,128)(2,1)S(1)}, bf16[128,256]{0,1:T(8,128)(2,1)S(1)}, u32[]{:S(2)}, u32[]{:S(2)}) collective-permute-start(bf16[128,256]{0,1:T(8,128)(2,1)S(1)} %collective-permute-done.8), channel_id=1, source_target_pairs={{0,1},{2,0},{4,2},{6,4},{7,6},{5,7},{3,5},{1,3},{8,9},{10,8},{12,1... | collective-permute-start | bytes 196616 | tf_op jit(solution)/shard_map/ppermute | solution.py:101
  62.6 4.3 %collective-permute-start.6 = (bf16[128,256]{0,1:T(8,128)(2,1)S(1)}, bf16[128,256]{0,1:T(8,128)(2,1)S(1)}, u32[]{:S(2)}, u32[]{:S(2)}) collective-permute-start(bf16[128,256]{0,1:T(8,128)(2,1)S(1)} %collective-permute-done.5), channel_id=1, source_target_pairs={{0,2},{2,4},{4,6},{6,7},{7,5},{5,3},{3,1},{1,0},{8,10},{10,12},{12... | collective-permute-start | bytes 196616 | tf_op jit(solution)/shard_map/ppermute | solution.py:101
  66.9 5.0 %collective-permute-start.14 = (bf16[2048,256]{1,0:T(8,128)(2,1)}, bf16[2048,256]{1,0:T(8,128)(2,1)S(1)}, u32[]{:S(2)}, u32[]{:S(2)}) collective-permute-start(bf16[2048,256]{1,0:T(8,128)(2,1)} %collective-permute-done.13), channel_id=1, source_target_pairs={{0,8},{8,0},{16,24},{24,16},{1,9},{9,1},{17,25},{25,17},{2,10},{10... | collective-permute-start | bytes 3145736 | tf_op jit(solution)/shard_map/ppermute | solution.py:128
  69.9 11.4 %copy-start.13 = (bf16[8192]{0:T(1024)(128)(2,1)S(1)}, bf16[8192]{0:T(1024)(128)(2,1)}, u32[]{:S(2)}) copy-start(bf16[8192]{0:T(1024)(128)(2,1)} %param.15) | copy-start | bytes 49156
  70.0 27.2 %copy-start.2 = (bf16[128,512]{1,0:T(8,128)(2,1)}, bf16[128,512]{1,0:T(8,128)(2,1)S(1)}, u32[]{:S(2)}) copy-start(bf16[128,512]{1,0:T(8,128)(2,1)S(1)} %pad_maximum_fusion.refs_4_) | copy-start | bytes 393220
  70.0 6.3 %collective-permute-start.11 = (bf16[128,512]{1,0:T(8,128)(2,1)S(1)}, bf16[128,512]{1,0:T(8,128)(2,1)S(1)}, u32[]{:S(2)}, u32[]{:S(2)}) collective-permute-start(bf16[128,512]{1,0:T(8,128)(2,1)S(1)} %pad_maximum_fusion.refs_4_), channel_id=1, source_target_pairs={{0,2},{2,4},{4,6},{6,7},{7,5},{5,3},{3,1},{1,0},{8,10},{10,12},{12... | collective-permute-start | bytes 393224 | tf_op jit(solution)/shard_map/ppermute | solution.py:101
  73.2 23.9 %copy-start.4 = (bf16[128,512]{1,0:T(8,128)(2,1)}, bf16[128,512]{1,0:T(8,128)(2,1)S(1)}, u32[]{:S(2)}) copy-start(bf16[128,512]{1,0:T(8,128)(2,1)S(1)} %pad_maximum_fusion.1.refs_5_) | copy-start | bytes 393220
  73.2 6.4 %collective-permute-start.21 = (bf16[128,512]{1,0:T(8,128)(2,1)S(1)}, bf16[128,512]{1,0:T(8,128)(2,1)S(1)}, u32[]{:S(2)}, u32[]{:S(2)}) collective-permute-start(bf16[128,512]{1,0:T(8,128)(2,1)S(1)} %pad_maximum_fusion.1.refs_5_), channel_id=1, source_target_pairs={{0,1},{2,0},{4,2},{6,4},{7,6},{5,7},{3,5},{1,3},{8,9},{10,8},{12,1... | collective-permute-start | bytes 393224 | tf_op jit(solution)/shard_map/ppermute | solution.py:101
  75.0 7.4 %collective-permute-start.12 = (bf16[128,512]{1,0:T(8,128)(2,1)S(1)}, bf16[128,512]{1,0:T(8,128)(2,1)S(1)}, u32[]{:S(2)}, u32[]{:S(2)}) collective-permute-start(bf16[128,512]{1,0:T(8,128)(2,1)S(1)} %pad_maximum_fusion.refs_4_), channel_id=1, source_target_pairs={{0,1},{2,0},{4,2},{6,4},{7,6},{5,7},{3,5},{1,3},{8,9},{10,8},{12,1... | collective-permute-start | bytes 393224 | tf_op jit(solution)/shard_map/ppermute | solution.py:101
  76.3 20.9 %copy-start.3 = (bf16[128,512]{1,0:T(8,128)(2,1)}, bf16[128,512]{1,0:T(8,128)(2,1)S(1)}, u32[]{:S(2)}) copy-start(bf16[128,512]{1,0:T(8,128)(2,1)S(1)} %collective-permute-done.11.refs_6_) | copy-start | bytes 393220
  76.3 7.9 %collective-permute-start.16 = (bf16[128,512]{1,0:T(8,128)(2,1)S(1)}, bf16[128,512]{1,0:T(8,128)(2,1)S(1)}, u32[]{:S(2)}, u32[]{:S(2)}) collective-permute-start(bf16[128,512]{1,0:T(8,128)(2,1)S(1)} %collective-permute-done.11.refs_6_), channel_id=1, source_target_pairs={{0,2},{2,4},{4,6},{6,7},{7,5},{5,3},{3,1},{1,0},{8,10},{10,12},{12... | collective-permute-start | bytes 393224 | tf_op jit(solution)/shard_map/ppermute | solution.py:101
  77.0 7.4 %collective-permute-start.15 = (bf16[128,512]{1,0:T(8,128)(2,1)S(1)}, bf16[128,512]{1,0:T(8,128)(2,1)S(1)}, u32[]{:S(2)}, u32[]{:S(2)}) collective-permute-start(bf16[128,512]{1,0:T(8,128)(2,1)S(1)} %pad_maximum_fusion.1.refs_5_), channel_id=1, source_target_pairs={{0,2},{2,4},{4,6},{6,7},{7,5},{5,3},{3,1},{1,0},{8,10},{10,12},{12... | collective-permute-start | bytes 393224 | tf_op jit(solution)/shard_map/ppermute | solution.py:101
  79.6 17.5 %copy-start.6 = (bf16[128,512]{1,0:T(8,128)(2,1)}, bf16[128,512]{1,0:T(8,128)(2,1)S(1)}, u32[]{:S(2)}) copy-start(bf16[128,512]{1,0:T(8,128)(2,1)S(1)} %collective-permute-done.21.refs_19_) | copy-start | bytes 393220
  79.6 5.9 %collective-permute-start.22 = (bf16[128,512]{1,0:T(8,128)(2,1)S(1)}, bf16[128,512]{1,0:T(8,128)(2,1)S(1)}, u32[]{:S(2)}, u32[]{:S(2)}) collective-permute-start(bf16[128,512]{1,0:T(8,128)(2,1)S(1)} %collective-permute-done.21.refs_19_), channel_id=1, source_target_pairs={{0,1},{2,0},{4,2},{6,4},{7,6},{5,7},{3,5},{1,3},{8,9},{10,8},{12,1... | collective-permute-start | bytes 393224 | tf_op jit(solution)/shard_map/ppermute | solution.py:101
  82.4 14.7 %copy-start.5 = (bf16[128,512]{1,0:T(8,128)(2,1)}, bf16[128,512]{1,0:T(8,128)(2,1)S(1)}, u32[]{:S(2)}) copy-start(bf16[128,512]{1,0:T(8,128)(2,1)S(1)} %collective-permute-done.12.refs_18_) | copy-start | bytes 393220
  82.4 6.4 %collective-permute-start.25 = (bf16[128,512]{1,0:T(8,128)(2,1)S(1)}, bf16[128,512]{1,0:T(8,128)(2,1)S(1)}, u32[]{:S(2)}, u32[]{:S(2)}) collective-permute-start(bf16[128,512]{1,0:T(8,128)(2,1)S(1)} %collective-permute-done.12.refs_18_), channel_id=1, source_target_pairs={{0,1},{2,0},{4,2},{6,4},{7,6},{5,7},{3,5},{1,3},{8,9},{10,8},{12,1... | collective-permute-start | bytes 393224 | tf_op jit(solution)/shard_map/ppermute | solution.py:101
  84.2 13.0 %copy-start.7 = (bf16[128,512]{1,0:T(8,128)(2,1)}, bf16[128,512]{1,0:T(8,128)(2,1)S(1)}, u32[]{:S(2)}) copy-start(bf16[128,512]{1,0:T(8,128)(2,1)S(1)} %collective-permute-done.16.refs_8_) | copy-start | bytes 393220
  84.2 6.4 %collective-permute-start.18 = (bf16[128,512]{1,0:T(8,128)(2,1)S(1)}, bf16[128,512]{1,0:T(8,128)(2,1)S(1)}, u32[]{:S(2)}, u32[]{:S(2)}) collective-permute-start(bf16[128,512]{1,0:T(8,128)(2,1)S(1)} %collective-permute-done.16.refs_8_), channel_id=1, source_target_pairs={{0,2},{2,4},{4,6},{6,7},{7,5},{5,3},{3,1},{1,0},{8,10},{10,12},{12... | collective-permute-start | bytes 393224 | tf_op jit(solution)/shard_map/ppermute | solution.py:101
  84.5 12.7 %copy-start.8 = (bf16[128,512]{1,0:T(8,128)(2,1)}, bf16[128,512]{1,0:T(8,128)(2,1)S(1)}, u32[]{:S(2)}) copy-start(bf16[128,512]{1,0:T(8,128)(2,1)S(1)} %collective-permute-done.15.refs_7_) | copy-start | bytes 393220
  84.5 7.0 %collective-permute-start.17 = (bf16[128,512]{1,0:T(8,128)(2,1)S(1)}, bf16[128,512]{1,0:T(8,128)(2,1)S(1)}, u32[]{:S(2)}, u32[]{:S(2)}) collective-permute-start(bf16[128,512]{1,0:T(8,128)(2,1)S(1)} %collective-permute-done.15.refs_7_), channel_id=1, source_target_pairs={{0,2},{2,4},{4,6},{6,7},{7,5},{5,3},{3,1},{1,0},{8,10},{10,12},{12... | collective-permute-start | bytes 393224 | tf_op jit(solution)/shard_map/ppermute | solution.py:101
  85.5 11.6 %copy-start.9 = (bf16[128,512]{1,0:T(8,128)(2,1)}, bf16[128,512]{1,0:T(8,128)(2,1)S(1)}, u32[]{:S(2)}) copy-start(bf16[128,512]{1,0:T(8,128)(2,1)S(1)} %collective-permute-done.22.refs_17_) | copy-start | bytes 393220
  85.5 6.3 %collective-permute-start.23 = (bf16[128,512]{1,0:T(8,128)(2,1)S(1)}, bf16[128,512]{1,0:T(8,128)(2,1)}, u32[]{:S(2)}, u32[]{:S(2)}) collective-permute-start(bf16[128,512]{1,0:T(8,128)(2,1)S(1)} %collective-permute-done.22.refs_17_), channel_id=1, source_target_pairs={{0,1},{2,0},{4,2},{6,4},{7,6},{5,7},{3,5},{1,3},{8,9},{10,8},{12,1... | collective-permute-start | bytes 393224 | tf_op jit(solution)/shard_map/ppermute | solution.py:101
  88.8 8.4 %copy-start.10 = (bf16[128,512]{1,0:T(8,128)(2,1)}, bf16[128,512]{1,0:T(8,128)(2,1)S(1)}, u32[]{:S(2)}) copy-start(bf16[128,512]{1,0:T(8,128)(2,1)S(1)} %collective-permute-done.25.refs_16_) | copy-start | bytes 393220
  88.8 5.8 %collective-permute-start.26 = (bf16[128,512]{1,0:T(8,128)(2,1)S(1)}, bf16[128,512]{1,0:T(8,128)(2,1)}, u32[]{:S(2)}, u32[]{:S(2)}) collective-permute-start(bf16[128,512]{1,0:T(8,128)(2,1)S(1)} %collective-permute-done.25.refs_16_), channel_id=1, source_target_pairs={{0,1},{2,0},{4,2},{6,4},{7,6},{5,7},{3,5},{1,3},{8,9},{10,8},{12,1... | collective-permute-start | bytes 393224 | tf_op jit(solution)/shard_map/ppermute | solution.py:101
  90.5 6.7 %copy-start.11 = (bf16[128,512]{1,0:T(8,128)(2,1)}, bf16[128,512]{1,0:T(8,128)(2,1)S(1)}, u32[]{:S(2)}) copy-start(bf16[128,512]{1,0:T(8,128)(2,1)S(1)} %collective-permute-done.18.refs_10_) | copy-start | bytes 393220
  90.5 5.1 %collective-permute-start.20 = (bf16[128,512]{1,0:T(8,128)(2,1)S(1)}, bf16[128,512]{1,0:T(8,128)(2,1)}, u32[]{:S(2)}, u32[]{:S(2)}) collective-permute-start(bf16[128,512]{1,0:T(8,128)(2,1)S(1)} %collective-permute-done.18.refs_10_), channel_id=1, source_target_pairs={{0,2},{2,4},{4,6},{6,7},{7,5},{5,3},{3,1},{1,0},{8,10},{10,12},{12... | collective-permute-start | bytes 393224 | tf_op jit(solution)/shard_map/ppermute | solution.py:101
  91.5 5.7 %copy-start.12 = (bf16[128,512]{1,0:T(8,128)(2,1)}, bf16[128,512]{1,0:T(8,128)(2,1)S(1)}, u32[]{:S(2)}) copy-start(bf16[128,512]{1,0:T(8,128)(2,1)S(1)} %collective-permute-done.17.refs_9_) | copy-start | bytes 393220
  91.5 5.5 %collective-permute-start.19 = (bf16[128,512]{1,0:T(8,128)(2,1)S(1)}, bf16[128,512]{1,0:T(8,128)(2,1)}, u32[]{:S(2)}, u32[]{:S(2)}) collective-permute-start(bf16[128,512]{1,0:T(8,128)(2,1)S(1)} %collective-permute-done.17.refs_9_), channel_id=1, source_target_pairs={{0,2},{2,4},{4,6},{6,7},{7,5},{5,3},{3,1},{1,0},{8,10},{10,12},{12... | collective-permute-start | bytes 393224 | tf_op jit(solution)/shard_map/ppermute | solution.py:101
  91.8 5.3 %collective-permute-start.24 = (bf16[128,512]{1,0:T(8,128)(2,1)}, bf16[128,512]{1,0:T(8,128)(2,1)}, u32[]{:S(2)}, u32[]{:S(2)}) collective-permute-start(bf16[128,512]{1,0:T(8,128)(2,1)} %collective-permute-done.23.refs_15_), channel_id=1, source_target_pairs={{0,1},{2,0},{4,2},{6,4},{7,6},{5,7},{3,5},{1,3},{8,9},{10,8},{12,1... | collective-permute-start | bytes 393224 | tf_op jit(solution)/shard_map/ppermute | solution.py:101
